TPU v7x, 512 devices: a whole 4x8x8 slice. The times are simulated.
512 devices in a mesh: gy: 8 (over x, core), gx: 64 (over z, y).
Axes of the slice: x: 4, y: 8, z: 8, core: 2. Of those that a mesh axis runs over, the one named last changes fastest.
Arguments:
- position: float32 [16, 512, 128, 3], P('gy', 'gx'), may hold values from 0 to 1
- velocity: float32 [16, 512, 128, 3], P('gy', 'gx'), may hold values from -6 to 6
- particle_mass: float32 [16, 512, 128], P('gy', 'gx'), may hold values from 0.006 to 0.025
- cell_counts: int32 [16, 512], P('gy', 'gx'), may hold values from 64 to 128
- shear_shift: int32 [1], replicated, may hold values from 252 to 260
Outputs:
- density: float32 [16, 512, 128], P('gy', 'gx')
- acceleration: float32 [16, 512, 128, 3], P('gy', 'gx')
Inputs may be any that keep to these rules, and one draw needn't show every extreme that they name: `shear_shift`: the offset is a whole number of cells from 252 to 260.
All inputs are finite; a program needn't handle non-finite values.
Results may differ from a plain program's by a relative error of at most 0.0003.
Values sent between devices are 32-bit elements; how exact they have to be, the bound alone decides.
A program may use at most 64 MiB of HBM per device.

v0:
```python
import math

import jax
import jax.numpy as jnp
from jax import lax
from jax.sharding import PartitionSpec as P

SMOOTHING = 0.5
KERNEL_NORM = 1.0 / (math.pi * SMOOTHING**3)
SOUND_SQ = 0.2
VISCOSITY = 0.05
SOFTENING = 0.0025
SHEAR_JUMP = 1.0


def with_halo(x, sides, width):
    for axis, dim in sides:
        peers, length = (lax.axis_size(axis), x.shape[dim])
        up = [(i, (i + 1) % peers) for i in range(peers)]
        down = [(j, i) for i, j in up]
        last = lax.slice_in_dim(x, length - width, length, axis=dim)
        first = lax.slice_in_dim(x, 0, width, axis=dim)
        before = lax.ppermute(last, axis, up)
        after = lax.ppermute(first, axis, down)
        x = jnp.concatenate([before, x, after], axis=dim)
    return x


def passed_along(x, axis, by):
    peers = lax.axis_size(axis)
    return lax.ppermute(x, axis, [(i, (i + by) % peers) for i in range(peers)])


def kernel_value(dist_sq):
    distance = jnp.sqrt(dist_sq)
    ratio = distance / SMOOTHING
    inner_part = 1.0 - 1.5 * ratio * ratio + 0.75 * ratio * ratio * ratio
    outer_part = 0.25 * jnp.maximum(2.0 - ratio, 0.0) ** 3
    return KERNEL_NORM * jnp.where(ratio < 1.0, inner_part, outer_part)


def kernel_slope(dist_sq):
    distance = jnp.sqrt(dist_sq)
    ratio = distance / SMOOTHING
    inner_part = (-3.0 + 2.25 * ratio) / (SMOOTHING * SMOOTHING)
    outer_part = (
        -0.75 * jnp.maximum(2.0 - ratio, 0.0) ** 2 / (SMOOTHING * jnp.maximum(distance, SMOOTHING))
    )
    return KERNEL_NORM * jnp.where(ratio < 1.0, inner_part, outer_part)


def stencil(padded, row_index):
    band = lax.dynamic_slice_in_dim(padded, row_index, 3, 0)
    columns = padded.shape[1] - 2
    cell_parts = []
    for up_down in range(3):
        for across in range(3):
            cell_parts.append(band[up_down, across : across + columns])
    return jnp.concatenate(cell_parts, axis=2)


def stencil_offsets(slots, dtype):
    parts = []
    for up_down in range(3):
        for across in range(3):
            entry = jnp.array([across - 1.0, up_down - 1.0, 0.0], dtype)
            parts.append(jnp.broadcast_to(entry[:, None], (3, slots)))
    return jnp.concatenate(parts, axis=1)


def own_cells(padded, row_index):
    return lax.dynamic_slice_in_dim(padded, row_index + 1, 1, 0)[0, 1:-1]


def pair_offsets(own_part, near_cells):
    shift_table = stencil_offsets(own_part.shape[2], near_cells.dtype)
    near_pos = near_cells[:, 0:3, :] + shift_table[None]
    return own_part[:, 0:3, :, None] - near_pos[:, :, None, :]


def densities(padded):

    def densities_one_row(row_index):
        near_cells = stencil(padded, row_index)
        own_part = own_cells(padded, row_index)
        offsets = pair_offsets(own_part, near_cells)
        dist_sq = jnp.sum(offsets * offsets, axis=1)
        return jnp.sum(near_cells[:, 6][:, None, :] * kernel_value(dist_sq), axis=-1)

    return lax.map(densities_one_row, jnp.arange(padded.shape[0] - 2, dtype=jnp.int32))


def forces(padded, rho_pad):
    rho_cells = rho_pad[:, :, None, :]

    def forces_one_row(row_index):
        near_cells = stencil(padded, row_index)
        near_rho = stencil(rho_cells, row_index)[:, 0][:, None, :]
        own_part = own_cells(padded, row_index)
        own_rho = own_cells(rho_cells, row_index)[:, 0][:, :, None]
        offsets = pair_offsets(own_part, near_cells)
        dist_sq = jnp.sum(offsets * offsets, axis=1)
        slope = kernel_slope(dist_sq)
        near_mass = near_cells[:, 6][:, None, :]
        pressure_term = -(SOUND_SQ / own_rho + SOUND_SQ / near_rho) * near_mass * slope
        viscous_term = (
            2.0
            * VISCOSITY
            * near_mass
            * slope
            * dist_sq
            / ((dist_sq + SOFTENING) * own_rho * near_rho)
        )
        relative = own_part[:, 3:6, :, None] - near_cells[:, 3:6, None, :]
        return jnp.sum(pressure_term[:, None] * offsets + viscous_term[:, None] * relative, axis=-1)

    return lax.map(forces_one_row, jnp.arange(padded.shape[0] - 2, dtype=jnp.int32))


def ghost_block(fields, ghost_width, shift_cells, vx_jump):
    columns = fields.shape[1]
    padded_y = with_halo(fields, (("gy", 0),), ghost_width)
    slab_index = lax.axis_index("gy")
    last_slab = lax.axis_size("gy") - 1
    total_columns = columns * lax.axis_size("gx")
    column_start = lax.axis_index("gx") * columns - ghost_width
    window = columns + 2 * ghost_width
    edge_rows = jnp.concatenate([padded_y[:ghost_width], padded_y[-ghost_width:]], axis=0)
    padded_xy = with_halo(padded_y, (("gx", 1),), ghost_width)
    half_cycle = lax.axis_size("gx") // 2
    far_parts = []
    for step in range(3):
        far_parts.append(passed_along(edge_rows, "gx", -(half_cycle - 1 + step)))
    near_rows = jnp.concatenate(far_parts, axis=1)
    base_column = (lax.axis_index("gx") + half_cycle - 1) * columns
    lower_start = (column_start + shift_cells - base_column) % total_columns
    upper_start = (column_start - shift_cells - base_column) % total_columns
    lower_far = lax.dynamic_slice_in_dim(near_rows[:ghost_width], lower_start, window, 1)
    upper_far = lax.dynamic_slice_in_dim(near_rows[ghost_width:], upper_start, window, 1)
    lower_rows = jnp.where(slab_index == 0, lower_far - vx_jump, padded_xy[:ghost_width])
    upper_rows = jnp.where(slab_index == last_slab, upper_far + vx_jump, padded_xy[-ghost_width:])
    return jnp.concatenate([lower_rows, padded_xy[ghost_width:-ghost_width], upper_rows], axis=0)


def local(position, velocity, particle_mass, cell_counts, shear_shift):
    shift_cells = shear_shift[0]
    slots = position.shape[2]
    is_valid = jnp.arange(slots, dtype=jnp.int32)[None, None, :] < cell_counts[:, :, None]
    weight = jnp.where(is_valid, particle_mass, 0.0)
    fields = jnp.concatenate(
        [
            jnp.transpose(position, (0, 1, 3, 2)),
            jnp.transpose(velocity, (0, 1, 3, 2)),
            weight[:, :, None, :],
        ],
        axis=2,
    )
    vx_jump = jnp.array([0.0, 0.0, 0.0, SHEAR_JUMP, 0.0, 0.0, 0.0], fields.dtype)[:, None]
    padded_two = ghost_block(fields, 2, shift_cells, vx_jump)
    cycle_rho = densities(padded_two)
    cycle_weight = padded_two[1:-1, 1:-1, 6, :]
    rho_pad = jnp.where(cycle_weight > 0.0, cycle_rho, 1.0)
    padded_one = padded_two[1:-1, 1:-1]
    density_raw = cycle_rho[1:-1, 1:-1]
    accel = jnp.transpose(forces(padded_one, rho_pad), (0, 1, 3, 2))
    density = jnp.where(is_valid, density_raw, 0.0)
    acceleration = jnp.where(is_valid[..., None], accel, 0.0)
    return (density, acceleration)


def solution(mesh):
    placed = (
        P("gy", "gx", None, None),
        P("gy", "gx", None, None),
        P("gy", "gx", None),
        P("gy", "gx"),
        P(),
    )
    return jax.shard_map(
        local,
        mesh=mesh,
        in_specs=placed,
        out_specs=(P("gy", "gx", None), P("gy", "gx", None, None)),
        check_vma=False,
    )
```

profile of v0, /device:TPU:191, one launch (start us, length us, event | category | flops | bytes accessed | tf_op | source)
XLA Modules:
  0.0 134.0 jit_solution(8340520923289944420)
XLA Ops:
  0.7 0.8 select_bitcast_fusion.1
  1.5 0.8 pad_maximum_fusion.2
  2.3 0.8 collective-permute-start
  3.1 0.8 iota_compare_fusion
  4.5 3.3 %collective-permute-done.1 = f32[2,8,7,128]{3,1,2,0:T(8,128)S(1)} collective-permute-done((f32[2,8,7,128]{3,1,2,0:T(8,128)S(1)}, f32[2,8,7,128]{3,1,2,0:T(8,128)S(1)}, u32[]{:S(2)}, u32[]{:S(2)}) %collective-permute-start.1) | collective-permute-done | bytes 57376 | tf_op jit(solution)/shard_map/ppermute | solution.py:24
  7.9 0.8 pad_maximum_fusion.7
  8.7 3.2 %collective-permute-start.5 = (f32[6,2,7,128]{3,1,2,0:T(2,128)S(1)}, f32[6,2,7,128]{3,1,2,0:T(2,128)S(1)}, u32[]{:S(2)}, u32[]{:S(2)}) collective-permute-start(f32[6,2,7,128]{3,1,2,0:T(2,128)S(1)} %get-tuple-element.455), channel_id=1, source_target_pairs={{0,1},{1,2},{2,3},{3,4},{4,5},{5,6},{6,7},{7,8},{8,9},{9,10},{10,1... | collective-permute-start | bytes 129032 | tf_op jit(solution)/shard_map/ppermute | solution.py:23
  11.9 2.1 %collective-permute-start.6 = (f32[6,2,7,128]{3,1,2,0:T(2,128)S(1)}, f32[6,2,7,128]{3,1,2,0:T(2,128)S(1)}, u32[]{:S(2)}, u32[]{:S(2)}) collective-permute-start(f32[6,2,7,128]{3,1,2,0:T(2,128)S(1)} %get-tuple-element.456), channel_id=1, source_target_pairs={{1,0},{2,1},{3,2},{4,3},{5,4},{6,5},{7,6},{8,7},{9,8},{10,9},{11,1... | collective-permute-start | bytes 129032 | tf_op jit(solution)/shard_map/ppermute | solution.py:24
  14.0 10.2 %collective-permute-start.2 = (f32[4,8,7,128]{3,1,2,0:T(8,128)S(1)}, f32[4,8,7,128]{3,1,2,0:T(8,128)S(1)}, u32[]{:S(2)}, u32[]{:S(2)}) collective-permute-start(f32[4,8,7,128]{3,1,2,0:T(8,128)S(1)} %constant_dynamic-update-slice_fusion.45), channel_id=1, source_target_pairs={{0,33},{1,34},{2,35},{3,36},{4,37},{5,38},{6,39},{7,40},{8,41},{9,... | collective-permute-start | bytes 344072 | tf_op jit(solution)/shard_map/ppermute | solution.py:31
  24.2 1.9 %collective-permute-start.3 = (f32[4,8,7,128]{3,1,2,0:T(8,128)S(1)}, f32[4,8,7,128]{3,1,2,0:T(8,128)S(1)}, u32[]{:S(2)}, u32[]{:S(2)}) collective-permute-start(f32[4,8,7,128]{3,1,2,0:T(8,128)S(1)} %constant_dynamic-update-slice_fusion.45), channel_id=1, source_target_pairs={{0,32},{1,33},{2,34},{3,35},{4,36},{5,37},{6,38},{7,39},{8,40},{9,... | collective-permute-start | bytes 344072 | tf_op jit(solution)/shard_map/ppermute | solution.py:31
  26.1 6.8 %collective-permute-start.4 = (f32[4,8,7,128]{3,1,2,0:T(8,128)S(1)}, f32[4,8,7,128]{3,1,2,0:T(8,128)S(1)}, u32[]{:S(2)}, u32[]{:S(2)}) collective-permute-start(f32[4,8,7,128]{3,1,2,0:T(8,128)S(1)} %constant_dynamic-update-slice_fusion.45), channel_id=1, source_target_pairs={{0,31},{1,32},{2,33},{3,34},{4,35},{5,36},{6,37},{7,38},{8,39},{9,... | collective-permute-start | bytes 344072 | tf_op jit(solution)/shard_map/ppermute | solution.py:31
  33.0 0.8 pad_maximum_fusion
  33.9 18.9 %collective-permute-done.3 = f32[4,8,7,128]{3,1,2,0:T(8,128)S(1)} collective-permute-done((f32[4,8,7,128]{3,1,2,0:T(8,128)S(1)}, f32[4,8,7,128]{3,1,2,0:T(8,128)S(1)}, u32[]{:S(2)}, u32[]{:S(2)}) %collective-permute-start.3) | collective-permute-done | bytes 114720 | tf_op jit(solution)/shard_map/ppermute | solution.py:31
  52.9 0.8 slice_select_fusion.1
  53.8 47.0 %while.28 = (s32[]{:T(128)}, f32[4,10,128]{2,1,0:T(8,128)S(1)}, s32[4]{0:T(128)S(1)}, f32[6,12,7,128]{3,1,2,0:T(8,128)S(1)}, f32[3]{0:T(128)S(1)}, /*index=5*/f3...) while((s32[]{:T(128)}, f32[4,10,128]{2,1,0:T(8,128)S(1)}, ...), condition=%wide.region_3.4_spmd.clone.clone, body=%wide.region_0.3_spmd.sunk.clone.sunk.clone | while | flops 36908812 | bytes 13842773 | solution.py:90
  53.8 0.6 dynamic_slice.80
  58.6 2.2 %multiply_reduce_fusion.3 = f32[10,128,1152]{2,1,0:T(8,128)S(1)} fusion(f32[10,3,1152]{2,1,0:T(4,128)S(1)} %copy.88, f32[10,3,128]{2,1,0:T(4,128)S(1)} %copy.89), kind=kLoop, calls=%fused_computation.clone.1.clone | loop fusion | flops 11796480 | bytes 6051840 | tf_op jit(solution)/shard_map/while/body/eval_jaxpr/reduce_sum | solution.py:87
  60.8 4.7 %fusion.61 = f32[10,128]{1,0:T(8,128)S(1)} fusion(f32[10,128,1152]{2,1,0:T(8,128)S(1)} %multiply_reduce_fusion.3, f32[10,1152]{1,0:T(8,128)S(1)} %fusion.60), kind=kLoop, calls=%fused_computation.6.clone.1.clone | loop fusion | flops 25066240 | bytes 5949440 | tf_op jit(solution)/shard_map/while/body/eval_jaxpr/reduce_sum | solution.py:88
  70.3 2.2 %multiply_reduce_fusion.3 = f32[10,128,1152]{2,1,0:T(8,128)S(1)} fusion(f32[10,3,1152]{2,1,0:T(4,128)S(1)} %copy.88, f32[10,3,128]{2,1,0:T(4,128)S(1)} %copy.89), kind=kLoop, calls=%fused_computation.clone.1.clone | loop fusion | flops 11796480 | bytes 6051840 | tf_op jit(solution)/shard_map/while/body/eval_jaxpr/reduce_sum | solution.py:87
  72.6 4.7 %fusion.61 = f32[10,128]{1,0:T(8,128)S(1)} fusion(f32[10,128,1152]{2,1,0:T(8,128)S(1)} %multiply_reduce_fusion.3, f32[10,1152]{1,0:T(8,128)S(1)} %fusion.60), kind=kLoop, calls=%fused_computation.6.clone.1.clone | loop fusion | flops 25066240 | bytes 5949440 | tf_op jit(solution)/shard_map/while/body/eval_jaxpr/reduce_sum | solution.py:88
  82.1 2.2 %multiply_reduce_fusion.3 = f32[10,128,1152]{2,1,0:T(8,128)S(1)} fusion(f32[10,3,1152]{2,1,0:T(4,128)S(1)} %copy.88, f32[10,3,128]{2,1,0:T(4,128)S(1)} %copy.89), kind=kLoop, calls=%fused_computation.clone.1.clone | loop fusion | flops 11796480 | bytes 6051840 | tf_op jit(solution)/shard_map/while/body/eval_jaxpr/reduce_sum | solution.py:87
  84.3 4.7 %fusion.61 = f32[10,128]{1,0:T(8,128)S(1)} fusion(f32[10,128,1152]{2,1,0:T(8,128)S(1)} %multiply_reduce_fusion.3, f32[10,1152]{1,0:T(8,128)S(1)} %fusion.60), kind=kLoop, calls=%fused_computation.6.clone.1.clone | loop fusion | flops 25066240 | bytes 5949440 | tf_op jit(solution)/shard_map/while/body/eval_jaxpr/reduce_sum | solution.py:88
  93.8 2.2 %multiply_reduce_fusion.3 = f32[10,128,1152]{2,1,0:T(8,128)S(1)} fusion(f32[10,3,1152]{2,1,0:T(4,128)S(1)} %copy.88, f32[10,3,128]{2,1,0:T(4,128)S(1)} %copy.89), kind=kLoop, calls=%fused_computation.clone.1.clone | loop fusion | flops 11796480 | bytes 6051840 | tf_op jit(solution)/shard_map/while/body/eval_jaxpr/reduce_sum | solution.py:87
  96.1 4.7 %fusion.61 = f32[10,128]{1,0:T(8,128)S(1)} fusion(f32[10,128,1152]{2,1,0:T(8,128)S(1)} %multiply_reduce_fusion.3, f32[10,1152]{1,0:T(8,128)S(1)} %fusion.60), kind=kLoop, calls=%fused_computation.6.clone.1.clone | loop fusion | flops 25066240 | bytes 5949440 | tf_op jit(solution)/shard_map/while/body/eval_jaxpr/reduce_sum | solution.py:88
  100.8 0.7 slice_select_fusion.2
  101.6 31.8 %while.29 = (s32[]{:T(128)}, f32[2,8,3,128]{3,1,2,0:T(8,128)S(1)}, s32[2]{0:T(128)S(1)}, f32[4,10,1,128]{3,1,2,0:T(8,128)S(1)}, f32[4,10,7,128]{3,1,2,0:T(8,128)...) while((s32[]{:T(128)}, f32[2,8,3,128]{3,1,2,0:T(8,128)S(1)}, ...), condition=%wide.region_7.8_spmd.clone.clone, body=%wide.region_4.7_spmd.sunk.clone.sunk.clone | while | flops 59026444 | bytes 30813660 | solution.py:117
  106.3 1.7 %fusion.63 = f32[8,128,1152]{2,1,0:T(8,128)S(1)} fusion(f32[8,3,1152]{2,1,0:T(4,128)S(1)} %copy.93, f32[8,3,128]{2,1,0:T(4,128)S(1)} %copy.94), kind=kLoop, calls=%fused_computation.43.clone.1.clone | loop fusion | flops 9437184 | bytes 4841472 | tf_op jit(solution)/shard_map/while/body/eval_jaxpr/reduce_sum | solution.py:102
  108.4 5.2 %multiply_multiply_fusion.5 = (f32[8,128,1152]{2,1,0:T(8,128)S(1)}, f32[8,128,1152]{2,1,0:T(8,128)S(1)}) fusion(f32[8,1152]{1,0:T(8,128)S(1)} %get-tuple-element.590, f32[8,1152]{1,0:T(8,128)S(1)} %broadcast_divide_fusion.7, f32[8,128]{1,0:T(8,128)S(1)} %get-tuple-element.592, f32[8,128,1152]{2,1,0:T(8,128)S(1)} %fusion.63, ...), kind=kLoop, calls=%fused_computation.47.clone.1.clone | loop fusion | flops 28311552 | bytes 14311424 | tf_op jit(solution)/shard_map/while/body/eval_jaxpr/mul | solution.py:105
  113.6 3.8 %fusion.64 = f32[8,3,128]{2,1,0:T(4,128)S(1)} fusion(f32[8,3,1152]{2,1,0:T(4,128)S(1)} %copy.91, f32[8,3,128]{2,1,0:T(4,128)S(1)} %copy.92, f32[8,128,1152]{2,1,0:T(8,128)S(1)} %get-tuple-element.597, f32[8,128,1152]{2,1,0:T(8,128)S(1)} %get-tuple-element.598, f32[8,3,1152]{2,1,0:T(4,128)S(1)} %copy.93, f32[8,3,128]{2,1,0:T(4,128)S(1)} %copy.94), kind=kLoop, calls=%fused_computation.45.clone.1.clone | loop fusion | flops 21230592 | bytes 9695232 | tf_op jit(solution)/shard_map/while/body/eval_jaxpr/reduce_sum | solution.py:115
  122.2 1.7 %fusion.63 = f32[8,128,1152]{2,1,0:T(8,128)S(1)} fusion(f32[8,3,1152]{2,1,0:T(4,128)S(1)} %copy.93, f32[8,3,128]{2,1,0:T(4,128)S(1)} %copy.94), kind=kLoop, calls=%fused_computation.43.clone.1.clone | loop fusion | flops 9437184 | bytes 4841472 | tf_op jit(solution)/shard_map/while/body/eval_jaxpr/reduce_sum | solution.py:102
  124.3 5.2 %multiply_multiply_fusion.5 = (f32[8,128,1152]{2,1,0:T(8,128)S(1)}, f32[8,128,1152]{2,1,0:T(8,128)S(1)}) fusion(f32[8,1152]{1,0:T(8,128)S(1)} %get-tuple-element.590, f32[8,1152]{1,0:T(8,128)S(1)} %broadcast_divide_fusion.7, f32[8,128]{1,0:T(8,128)S(1)} %get-tuple-element.592, f32[8,128,1152]{2,1,0:T(8,128)S(1)} %fusion.63, ...), kind=kLoop, calls=%fused_computation.47.clone.1.clone | loop fusion | flops 28311552 | bytes 14311424 | tf_op jit(solution)/shard_map/while/body/eval_jaxpr/mul | solution.py:105
  129.5 3.8 %fusion.64 = f32[8,3,128]{2,1,0:T(4,128)S(1)} fusion(f32[8,3,1152]{2,1,0:T(4,128)S(1)} %copy.91, f32[8,3,128]{2,1,0:T(4,128)S(1)} %copy.92, f32[8,128,1152]{2,1,0:T(8,128)S(1)} %get-tuple-element.597, f32[8,128,1152]{2,1,0:T(8,128)S(1)} %get-tuple-element.598, f32[8,3,1152]{2,1,0:T(4,128)S(1)} %copy.93, f32[8,3,128]{2,1,0:T(4,128)S(1)} %copy.94), kind=kLoop, calls=%fused_computation.45.clone.1.clone | loop fusion | flops 21230592 | bytes 9695232 | tf_op jit(solution)/shard_map/while/body/eval_jaxpr/reduce_sum | solution.py:115
  (237 shorter events, 9.7 us)
Async XLA Ops:
  0.6 53.1 %copy-start = (f32[3]{0:T(128)S(1)}, f32[3]{0:T(128)}, u32[]{:S(2)}) copy-start(f32[3]{0:T(128)} %constant.227.clone..sunk.4) | copy-start | bytes 40
  0.6 53.1 %copy-start.1 = (f32[3]{0:T(128)S(1)}, f32[3]{0:T(128)}, u32[]{:S(2)}) copy-start(f32[3]{0:T(128)} %constant.228.clone..sunk.4) | copy-start | bytes 40
  0.7 53.1 %copy-start.2 = (f32[3]{0:T(128)S(1)}, f32[3]{0:T(128)}, u32[]{:S(2)}) copy-start(f32[3]{0:T(128)} %constant.229.clone..sunk.4) | copy-start | bytes 40
  0.7 53.1 %copy-start.3 = (f32[3]{0:T(128)S(1)}, f32[3]{0:T(128)}, u32[]{:S(2)}) copy-start(f32[3]{0:T(128)} %constant.230.clone..sunk.4) | copy-start | bytes 40
  0.7 53.1 %copy-start.4 = (f32[3]{0:T(128)S(1)}, f32[3]{0:T(128)}, u32[]{:S(2)}) copy-start(f32[3]{0:T(128)} %constant.232.clone..sunk.4) | copy-start | bytes 40
  0.7 53.1 %copy-start.5 = (f32[3]{0:T(128)S(1)}, f32[3]{0:T(128)}, u32[]{:S(2)}) copy-start(f32[3]{0:T(128)} %constant.233.clone..sunk.4) | copy-start | bytes 40
  0.7 53.1 %copy-start.6 = (f32[3]{0:T(128)S(1)}, f32[3]{0:T(128)}, u32[]{:S(2)}) copy-start(f32[3]{0:T(128)} %constant.234.clone..sunk.4) | copy-start | bytes 40
  0.7 53.1 %copy-start.7 = (f32[3]{0:T(128)S(1)}, f32[3]{0:T(128)}, u32[]{:S(2)}) copy-start(f32[3]{0:T(128)} %constant.235.clone..sunk.4) | copy-start | bytes 40
  2.3 2.2 %collective-permute-start = (f32[2,8,7,128]{3,1,2,0:T(8,128)S(1)}, f32[2,8,7,128]{3,1,2,0:T(8,128)S(1)}, u32[]{:S(2)}, u32[]{:S(2)}) collective-permute-start(f32[2,8,7,128]{3,1,2,0:T(8,128)S(1)} %pad_maximum_fusion.2), channel_id=1, source_target_pairs={{0,64},{64,128},{128,192},{192,256},{256,320},{320,384},{384,448},... | collective-permute-start | bytes 172040 | tf_op jit(solution)/shard_map/ppermute | solution.py:23
  3.0 4.8 %collective-permute-start.1 = (f32[2,8,7,128]{3,1,2,0:T(8,128)S(1)}, f32[2,8,7,128]{3,1,2,0:T(8,128)S(1)}, u32[]{:S(2)}, u32[]{:S(2)}) collective-permute-start(f32[2,8,7,128]{3,1,2,0:T(8,128)S(1)} %pad_maximum_fusion.2), channel_id=1, source_target_pairs={{64,0},{128,64},{192,128},{256,192},{320,256},{384,320},{448,384},... | collective-permute-start | bytes 172040 | tf_op jit(solution)/shard_map/ppermute | solution.py:24
  8.7 24.3 %collective-permute-start.5 = (f32[6,2,7,128]{3,1,2,0:T(2,128)S(1)}, f32[6,2,7,128]{3,1,2,0:T(2,128)S(1)}, u32[]{:S(2)}, u32[]{:S(2)}) collective-permute-start(f32[6,2,7,128]{3,1,2,0:T(2,128)S(1)} %get-tuple-element.455), channel_id=1, source_target_pairs={{0,1},{1,2},{2,3},{3,4},{4,5},{5,6},{6,7},{7,8},{8,9},{9,10},{10,1... | collective-permute-start | bytes 129032 | tf_op jit(solution)/shard_map/ppermute | solution.py:23
  11.9 21.1 %collective-permute-start.6 = (f32[6,2,7,128]{3,1,2,0:T(2,128)S(1)}, f32[6,2,7,128]{3,1,2,0:T(2,128)S(1)}, u32[]{:S(2)}, u32[]{:S(2)}) collective-permute-start(f32[6,2,7,128]{3,1,2,0:T(2,128)S(1)} %get-tuple-element.456), channel_id=1, source_target_pairs={{1,0},{2,1},{3,2},{4,3},{5,4},{6,5},{7,6},{8,7},{9,8},{10,9},{11,1... | collective-permute-start | bytes 129032 | tf_op jit(solution)/shard_map/ppermute | solution.py:24
  14.0 19.8 %collective-permute-start.2 = (f32[4,8,7,128]{3,1,2,0:T(8,128)S(1)}, f32[4,8,7,128]{3,1,2,0:T(8,128)S(1)}, u32[]{:S(2)}, u32[]{:S(2)}) collective-permute-start(f32[4,8,7,128]{3,1,2,0:T(8,128)S(1)} %constant_dynamic-update-slice_fusion.45), channel_id=1, source_target_pairs={{0,33},{1,34},{2,35},{3,36},{4,37},{5,38},{6,39},{7,40},{8,41},{9,... | collective-permute-start | bytes 344072 | tf_op jit(solution)/shard_map/ppermute | solution.py:31
  24.2 28.6 %collective-permute-start.3 = (f32[4,8,7,128]{3,1,2,0:T(8,128)S(1)}, f32[4,8,7,128]{3,1,2,0:T(8,128)S(1)}, u32[]{:S(2)}, u32[]{:S(2)}) collective-permute-start(f32[4,8,7,128]{3,1,2,0:T(8,128)S(1)} %constant_dynamic-update-slice_fusion.45), channel_id=1, source_target_pairs={{0,32},{1,33},{2,34},{3,35},{4,36},{5,37},{6,38},{7,39},{8,40},{9,... | collective-permute-start | bytes 344072 | tf_op jit(solution)/shard_map/ppermute | solution.py:31
  26.1 26.7 %collective-permute-start.4 = (f32[4,8,7,128]{3,1,2,0:T(8,128)S(1)}, f32[4,8,7,128]{3,1,2,0:T(8,128)S(1)}, u32[]{:S(2)}, u32[]{:S(2)}) collective-permute-start(f32[4,8,7,128]{3,1,2,0:T(8,128)S(1)} %constant_dynamic-update-slice_fusion.45), channel_id=1, source_target_pairs={{0,31},{1,32},{2,33},{3,34},{4,35},{5,36},{6,37},{7,38},{8,39},{9,... | collective-permute-start | bytes 344072 | tf_op jit(solution)/shard_map/ppermute | solution.py:31
  53.8 47.0 %copy-start.8 = (s32[2,8]{1,0:T(2,128)S(1)}, s32[2,8]{1,0:T(2,128)}, u32[]{:S(2)}) copy-start(s32[2,8]{1,0:T(2,128)} %param.31) | copy-start | bytes 196
where the time goes:
time: 135 us; the launch traced here: 134 us
  other arithmetic  55.5 us (41%)
  starting transfers between devices  25 us (19%)
  waiting for transfers between devices  22.3 us (17%)
  loops' own time  20.2 us (15%)
  local copies, waits for them, and re-layouts  9.4 us (7%)
  between operations  1.7 us (1%)
    ppermute x3, waiting for transfers between devices, passed_along(): return lax.ppermute(x, axis, [(i, (i + by) % peers) for i in range(peers)])  18.9 us
    ppermute x3, starting transfers between devices, passed_along(): return lax.ppermute(x, axis, [(i, (i + by) % peers) for i in range(peers)])  18.9 us
    reduce_sum x4, other arithmetic, densities_one_row(): jnp.sum(near_cells[:, 6][:, None, :] * kernel_value(dist_sq), axis=-1)  18.9 us
    another operation x1, loops' own time, densities(): lax.map(densities_one_row, jnp.arange(padded.shape[0] - 2, dtype=jnp.int32))  13.3 us
    mul x4, other arithmetic, forces_one_row(): -(SOUND_SQ / own_rho + SOUND_SQ / near_rho) * near_mass * slope  10.4 us
    reduce_sum x4, other arithmetic, densities_one_row(): dist_sq = jnp.sum(offsets * offsets, axis=1)  8.8 us
    reduce_sum x2, other arithmetic, forces_one_row(): jnp.sum(pressure_term[:, None] * offsets + viscous_term[:, None] * relati...  7.69 us
    another operation x1, loops' own time, forces(): lax.map(forces_one_row, jnp.arange(padded.shape[0] - 2, dtype=jnp.int32))  6.97 us
  transfers between devices with their start and end apart: 7, of which 2 were waited for; matrix products, arithmetic and copies ran while one was open for 1% of the time, Pallas kernels for 0%

commit v1 on v0

v1 whole, which is shorter than its diff:
```python
import functools
import math

import jax
import jax.numpy as jnp
from jax import lax
from jax.experimental import pallas as pl
from jax.experimental.pallas import tpu as pltpu
from jax.sharding import PartitionSpec as P

SMOOTHING = 0.5
KERNEL_NORM = 1.0 / (math.pi * SMOOTHING**3)
SOUND_SQ = 0.2
VISCOSITY = 0.05
SOFTENING = 0.0025
SHEAR_JUMP = 1.0

MESH = pl.DeviceIdType.MESH
F32 = jnp.float32
BF16 = jnp.bfloat16
RHO_SCALE = KERNEL_NORM * 0.25
GRAD_SCALE = KERNEL_NORM * 0.75 / (SMOOTHING * SMOOTHING)
SOFT_Q = SOFTENING / (SMOOTHING * SMOOTHING)
TINY_Q = 1e-8
SLOTS = 128
ROWS = 2
COLS = 8
EDGE = 5
WINDOW = 2 * EDGE + COLS


def pieces(p):
    high = p.astype(BF16).astype(F32)
    rest = p - high
    middle = rest.astype(BF16).astype(F32)
    return high, middle, rest - middle


def zeros(n):
    return jnp.zeros((n, SLOTS), F32)


def kernel(
    ny, nx,
    counts, shift, pos, vel, mass,
    dens_out, acc_out,
    own_a, own_v, own_m,
    below_a, below_v, below_m,
    above_a, above_v, above_m,
    side_a, side_v, side_m,
    near, centre, feats, mass_cols,
    g_high, g_low, e_part,
    rho_part, sums,
    send_sem, recv_sem,
):
    gy, gx = lax.axis_index("gy"), lax.axis_index("gx")
    top = gy // (ny - 1)
    bottom = (ny - 1 - gy) // (ny - 1)
    half = nx // 2
    up_y, down_y = lax.rem(gy + 1, ny), lax.rem(gy + ny - 1, ny)

    def up_id(k):
        return (up_y, lax.rem(gx + half * top + k + nx, nx))

    def down_id(k):
        return (down_y, lax.rem(gx + half * bottom + k + nx, nx))

    left_id = (gy, lax.rem(gx + nx - 1, nx))
    right_id = (gy, lax.rem(gx + 1, nx))

    row_a, row_v, row_m = (below_a, above_a), (below_v, above_v), (below_m, above_m)
    barrier = pltpu.get_barrier_semaphore()
    for k in (0, -1, 1):
        pl.semaphore_signal(barrier, inc=1, device_id=up_id(k), device_id_type=MESH)
        pl.semaphore_signal(barrier, inc=1, device_id=down_id(k), device_id_type=MESH)
    pl.semaphore_signal(barrier, inc=1, device_id=left_id, device_id_type=MESH)
    pl.semaphore_signal(barrier, inc=1, device_id=right_id, device_id_type=MESH)

    def copy_of(phase, slot, src, dst, device):
        return pltpu.make_async_remote_copy(
            src_ref=src,
            dst_ref=dst,
            send_sem=send_sem.at[phase, slot],
            recv_sem=recv_sem.at[phase, slot],
            device_id=device,
            device_id_type=MESH,
        )

    spans = {
        1: (COLS - EDGE, EDGE, 0),
        0: (0, COLS, EDGE),
        -1: (0, EDGE, EDGE + COLS),
    }

    def copies(phase, own, row, side):
        out = []
        for k in (0, -1, 1):
            start, count, at = spans[k]
            out.append(copy_of(phase, 1 - k, own.at[1, pl.ds(start, count)], row[0].at[pl.ds(at, count)], up_id(k)))
            out.append(copy_of(phase, 4 - k, own.at[0, pl.ds(start, count)], row[1].at[pl.ds(at, count)], down_id(k)))
        out.append(copy_of(phase, 6, own.at[:, COLS - 1], side.at[0], right_id))
        out.append(copy_of(phase, 7, own.at[:, 0], side.at[1], left_id))
        return out

    def wait_row(phase, own, row, d):
        for k in (0, -1, 1):
            start, count, at = spans[k]
            copy_of(phase, 3 * d + 1 - k, own.at[0, pl.ds(start, count)], row[d].at[pl.ds(at, count)], left_id).wait_recv()

    def wait_side(phase, own, side):
        for s in (0, 1):
            copy_of(phase, 6 + s, own.at[:, 0], side.at[s], left_id).wait_recv()

    lane = lax.broadcasted_iota(jnp.int32, (COLS, SLOTS), 1)
    column = lax.broadcasted_iota(jnp.int32, (COLS, SLOTS), 0).astype(F32)

    def valid_of(r):
        bound = jnp.concatenate([jnp.full((1, SLOTS), counts[r, c], jnp.int32) for c in range(COLS)], axis=0)
        return lane < bound

    for r in range(ROWS):
        fields = [pos[r, 0], pos[r, 1], pos[r, 2], jnp.where(valid_of(r), mass[r], 0.0)]
        for f in range(4):
            for c in range(COLS):
                own_a[r, c, f : f + 1, :] = fields[f][c : c + 1, :]
        for f in range(3):
            for c in range(COLS):
                own_v[r, c, f : f + 1, :] = vel[r, f][c : c + 1, :]
        for c in range(COLS):
            own_v[r, c, 3:4, :] = zeros(1)

    def prepare(e, j, xyzw):
        e_f = e.astype(F32) if hasattr(e, "astype") else float(e)
        x = 2.0 * xyzw[0:1] + (2.0 * j - 10.0)
        y = 2.0 * xyzw[1:2] + (2.0 * e_f - 4.0)
        z = 2.0 * xyzw[2:3] - 1.0
        w = xyzw[3:4]
        n = x * x + y * y + z * z
        one = jnp.ones((1, SLOTS), F32)
        lhs = jnp.concatenate([x, y, z, n, one, w, zeros(2)], axis=0)
        high, middle, low = pieces(lhs)
        table = jnp.concatenate([high, high, high, middle, middle, low, lhs, zeros(8)], axis=0).T
        near[e, j * SLOTS : (j + 1) * SLOTS, :] = table.astype(BF16)
        mass_cols[e, j * SLOTS : (j + 1) * SLOTS, :] = jnp.broadcast_to(table[:, 53:54], (SLOTS, SLOTS))
        first = jnp.concatenate([w, w * x, w * y, w * z, zeros(4)], axis=0)
        feats[e, 32:64, j * SLOTS : (j + 1) * SLOTS] = jnp.concatenate([*pieces(first), zeros(8)], axis=0).astype(BF16)
        return x, y, z, n, one

    def prepare_own(r, carry):
        for c in range(COLS):
            x, y, z, n, one = prepare(r + 1, c + 1, own_a[r, c])
            rhs = jnp.concatenate([-2.0 * x, -2.0 * y, -2.0 * z, one, n, zeros(3)], axis=0)
            high, middle, low = pieces(rhs)
            centre[r, c] = jnp.concatenate([high, middle, low, high, middle, high, zeros(16)], axis=0).astype(BF16)
        return carry

    lax.fori_loop(0, ROWS, prepare_own, 0)
    rho_part[...] = jnp.zeros_like(rho_part)
    sums[...] = jnp.zeros_like(sums)

    pl.semaphore_wait(barrier, 8)
    sent = copies(0, own_a, row_a, side_a) + copies(1, own_v, row_v, side_v)
    for copy in sent:
        copy.start()

    def pairs(r, a, c):
        e = r + a
        total = rho_part[r, c]
        rhs = centre[r, c]
        for b in range(3):
            at = (c + b) * SLOTS
            q_sq = jnp.dot(near[e, at : at + SLOTS, :], rhs, preferred_element_type=F32)
            q_sq = jnp.maximum(q_sq, TINY_Q)
            inverse = lax.rsqrt(q_sq)
            q = q_sq * inverse
            u = jnp.maximum(2.0 - q, 0.0)
            s = jnp.maximum(1.0 - q, 0.0)
            u_sq = u * u
            s_sq = 4.0 * (s * s)
            value = u_sq * u - s_sq * s
            slope = (s_sq - u_sq) * inverse
            soft = lax.rsqrt(q_sq + SOFT_Q)
            extra = (slope * soft) * soft
            weighted = value * mass_cols[e, at : at + SLOTS, :]
            total = total + jnp.sum(weighted.reshape(SLOTS // 8, 8, SLOTS), axis=0)
            high = slope.astype(BF16)
            span = pl.ds(b * SLOTS, SLOTS)
            g_high[r, a, c, span, :] = high
            g_low[r, a, c, span, :] = (slope - high.astype(F32)).astype(BF16)
            e_part[r, a, c, span, :] = extra.astype(BF16)
        rho_part[r, c] = total

    def reduce(r, a, c):
        e = r + a
        lanes = pl.ds(c * SLOTS, 3 * SLOTS)
        rows = feats[e, :, lanes]
        g = jnp.dot(rows, g_high[r, a, c], preferred_element_type=F32)
        g = g + jnp.dot(rows, g_low[r, a, c], preferred_element_type=F32)
        v = jnp.dot(rows[0:32], e_part[r, a, c], preferred_element_type=F32)
        sums[r, c, 0:8, :] += g[0:8] + g[8:16] + g[16:24]
        sums[r, c, 8:16, :] += g[32:40] + g[40:48] + g[48:56]
        sums[r, c, 16:24, :] += v[0:8] + v[8:16] + v[16:24]

    def own_units(work, cells):
        def body(t, carry):
            r = t // 2
            a = 1 - r + lax.rem(t, 2)
            for c in cells:
                work(r, a, c)
            return carry

        lax.fori_loop(0, 4, body, 0)

    inner, outer = tuple(range(1, COLS - 1)), (0, COLS - 1)
    own_units(pairs, inner)
    wait_side(0, own_a, side_a)
    for s in (0, 1):
        for r in range(ROWS):
            prepare(r + 1, (COLS + 1) * s, side_a[s, r])
    own_units(pairs, outer)

    s_cells = shift[0]
    base = EDGE - 1
    drift = jnp.clip(s_cells - half * COLS, -base, base)

    starts = (base + bottom * drift, base - top * drift)

    def both_rows(work):
        pl.when(bottom == 1)(lambda: work(1))
        work(0)
        pl.when(bottom == 0)(lambda: work(1))

    def ghost_pairs(d):
        wait_row(0, own_a, row_a, d)
        for j in range(COLS + 2):
            prepare(3 * d, j, row_a[d][starts[d] + j])
        for c in range(COLS):
            pairs(d, 2 * d, c)

    both_rows(ghost_pairs)

    valid = [valid_of(r) for r in range(ROWS)]
    inverse_rho = []
    for r in range(ROWS):
        rho = jnp.concatenate([jnp.sum(rho_part[r, c], axis=0, keepdims=True) for c in range(COLS)], axis=0) * RHO_SCALE
        dens_out[r] = jnp.where(valid[r], rho, 0.0)
        inv = 1.0 / jnp.where(valid[r], rho, 1.0)
        inverse_rho.append(inv)
        ratio = jnp.where(valid[r], mass[r], 0.0) * inv
        for c in range(COLS):
            own_m[r, c] = ratio[c : c + 1, :]
    sent_m = copies(2, own_m, row_m, side_m)
    for copy in sent_m:
        copy.start()

    def second(e, j, xyzw, v, ratio, jump):
        e_f = e.astype(F32) if hasattr(e, "astype") else float(e)
        x = 2.0 * xyzw[0:1] + (2.0 * j - 10.0)
        y = 2.0 * xyzw[1:2] + (2.0 * e_f - 4.0)
        z = 2.0 * xyzw[2:3] - 1.0
        block = jnp.concatenate(
            [ratio, ratio * x, ratio * y, ratio * z, ratio * (v[0:1] + jump), ratio * v[1:2], ratio * v[2:3], zeros(1)],
            axis=0,
        )
        feats[e, 0:32, j * SLOTS : (j + 1) * SLOTS] = jnp.concatenate([*pieces(block), zeros(8)], axis=0).astype(BF16)

    def second_own(r, carry):
        for c in range(COLS):
            second(r + 1, c + 1, own_a[r, c], own_v[r, c], own_m[r, c], 0.0)
        return carry

    lax.fori_loop(0, ROWS, second_own, 0)
    own_units(reduce, inner)
    wait_side(1, own_v, side_v)
    wait_side(2, own_m, side_m)
    for s in (0, 1):
        for r in range(ROWS):
            second(r + 1, (COLS + 1) * s, side_a[s, r], side_v[s, r], side_m[s, r], 0.0)
    own_units(reduce, outer)

    jumps = (-(bottom.astype(F32)) * SHEAR_JUMP, top.astype(F32) * SHEAR_JUMP)

    def ghost_reduce(d):
        wait_row(1, own_v, row_v, d)
        wait_row(2, own_m, row_m, d)
        for j in range(COLS + 2):
            at = starts[d] + j
            second(3 * d, j, row_a[d][at], row_v[d][at], row_m[d][at], jumps[d])
        for c in range(COLS):
            reduce(d, 2 * d, c)

    both_rows(ghost_reduce)

    for r in range(ROWS):
        def row_of(k):
            return jnp.concatenate([sums[r, c, k : k + 1, :] for c in range(COLS)], axis=0)

        scaled = [
            2.0 * pos[r, 0] + (2.0 * column - 8.0),
            2.0 * pos[r, 1] + (2.0 * r - 2.0),
            2.0 * pos[r, 2] - 1.0,
        ]
        inv = inverse_rho[r]
        ratio_sum, mass_sum = row_of(0), row_of(8)
        visc_sum = ratio_sum - SOFT_Q * row_of(16)
        for f in range(3):
            far = scaled[f] * ratio_sum - row_of(1 + f)
            near_part = scaled[f] * mass_sum - row_of(9 + f)
            drag = vel[r, f] * visc_sum - (row_of(4 + f) - SOFT_Q * row_of(20 + f))
            total = (-0.5 * SOUND_SQ * GRAD_SCALE) * (inv * near_part + far) + (2.0 * VISCOSITY * GRAD_SCALE) * (inv * drag)
            acc_out[r, f] = jnp.where(valid[r], total, 0.0)

    for copy in sent + sent_m:
        copy.wait_send()


def local(ny, nx, position, velocity, particle_mass, cell_counts, shear_shift):
    pos = jnp.transpose(position, (0, 3, 1, 2))
    vel = jnp.transpose(velocity, (0, 3, 1, 2))
    vmem = pl.BlockSpec(memory_space=pltpu.VMEM)
    smem = pl.BlockSpec(memory_space=pltpu.SMEM)
    table = (ROWS, 3, COLS, 3 * SLOTS, SLOTS)
    density, accel = pl.pallas_call(
        functools.partial(kernel, ny, nx),
        out_shape=(
            jax.ShapeDtypeStruct((ROWS, COLS, SLOTS), F32),
            jax.ShapeDtypeStruct((ROWS, 3, COLS, SLOTS), F32),
        ),
        in_specs=[smem, smem, vmem, vmem, vmem],
        out_specs=(vmem, vmem),
        scratch_shapes=[
            pltpu.VMEM((ROWS, COLS, 4, SLOTS), F32),
            pltpu.VMEM((ROWS, COLS, 4, SLOTS), F32),
            pltpu.VMEM((ROWS, COLS, 1, SLOTS), F32),
            pltpu.VMEM((WINDOW, 4, SLOTS), F32),
            pltpu.VMEM((WINDOW, 4, SLOTS), F32),
            pltpu.VMEM((WINDOW, 1, SLOTS), F32),
            pltpu.VMEM((WINDOW, 4, SLOTS), F32),
            pltpu.VMEM((WINDOW, 4, SLOTS), F32),
            pltpu.VMEM((WINDOW, 1, SLOTS), F32),
            pltpu.VMEM((2, ROWS, 4, SLOTS), F32),
            pltpu.VMEM((2, ROWS, 4, SLOTS), F32),
            pltpu.VMEM((2, ROWS, 1, SLOTS), F32),
            pltpu.VMEM((ROWS + 2, (COLS + 2) * SLOTS, 64), BF16),
            pltpu.VMEM((ROWS, COLS, 64, SLOTS), BF16),
            pltpu.VMEM((ROWS + 2, 64, (COLS + 2) * SLOTS), BF16),
            pltpu.VMEM((ROWS + 2, (COLS + 2) * SLOTS, SLOTS), F32),
            pltpu.VMEM(table, BF16),
            pltpu.VMEM(table, BF16),
            pltpu.VMEM(table, BF16),
            pltpu.VMEM((ROWS, COLS, 8, SLOTS), F32),
            pltpu.VMEM((ROWS, COLS, 24, SLOTS), F32),
            pltpu.SemaphoreType.DMA((3, 8)),
            pltpu.SemaphoreType.DMA((3, 8)),
        ],
        compiler_params=pltpu.CompilerParams(
            collective_id=0, has_side_effects=True, vmem_limit_bytes=48 * 1024 * 1024
        ),
        name="sph_step",
    )(cell_counts, shear_shift, pos, vel, particle_mass)
    return density, jnp.transpose(accel, (0, 2, 3, 1))


def solution(mesh):
    placed = (
        P("gy", "gx", None, None),
        P("gy", "gx", None, None),
        P("gy", "gx", None),
        P("gy", "gx"),
        P(),
    )
    return jax.shard_map(
        functools.partial(local, mesh.shape["gy"], mesh.shape["gx"]),
        mesh=mesh,
        in_specs=placed,
        out_specs=(P("gy", "gx", None), P("gy", "gx", None, None)),
        check_vma=False,
    )
```

time: 135 us -> 37 us (0.27)
  the two profiles are of different devices: /device:TPU:191 before, /device:TPU:7 now
where the time goes in v1:
time: 37 us; the launch traced here: 36.7 us
  Pallas kernels  31.3 us (85%)
  local copies, waits for them, and re-layouts  4.05 us (11%)
  between operations  1.3 us (4%)
    pallas_call x1, Pallas kernels, local(): pl.pallas_call(functools.partial(kernel, ny, nx), out_shape=(jax.ShapeDty...  31.3 us
    unnamed x10, local copies, waits for them, and re-layouts  4.05 us

profile of v1, /device:TPU:7, one launch (start us, length us, event | category | flops | bytes accessed | tf_op | source)
XLA Modules:
  0.0 36.7 jit_solution(11472481356108041440)
XLA Ops:
  1.3 0.0 copy-start.3
  1.3 0.7 %copy-done.3 = s32[2,8]{1,0:T(2,128)S(1)} copy-done((s32[2,8]{1,0:T(2,128)S(1)}, s32[2,8]{1,0:T(2,128)}, u32[]{:S(2)}) %copy-start.3) | copy-done | bytes 88
  2.0 0.0 copy-start
  2.0 0.7 %copy-done = f32[2,8,128,3]{2,1,3,0:T(8,128)S(1)} copy-done((f32[2,8,128,3]{2,1,3,0:T(8,128)S(1)}, f32[2,8,128,3]{2,1,3,0:T(8,128)}, u32[]{:S(2)}) %copy-start) | copy-done | bytes 24600
  2.7 0.0 copy-start.1
  2.7 0.7 %copy-done.1 = f32[2,8,128,3]{2,1,3,0:T(8,128)S(1)} copy-done((f32[2,8,128,3]{2,1,3,0:T(8,128)S(1)}, f32[2,8,128,3]{2,1,3,0:T(8,128)}, u32[]{:S(2)}) %copy-start.1) | copy-done | bytes 24600
  3.4 0.0 copy-start.2
  3.4 0.7 %copy-done.2 = f32[2,8,128]{2,1,0:T(8,128)S(1)} copy-done((f32[2,8,128]{2,1,0:T(8,128)S(1)}, f32[2,8,128]{2,1,0:T(8,128)}, u32[]{:S(2)}) %copy-start.2) | copy-done | bytes 8216
  4.1 31.3 %sph_step.1 = (f32[2,8,128]{2,1,0:T(8,128)S(1)}, f32[2,3,8,128]{3,2,1,0:T(8,128)S(1)}) custom-call(s32[2,8]{1,0:T(2,128)S(1)} %copy-done.3, s32[1]{0:T(128)S(6)} %copy.9.shift, f32[2,3,8,128]{3,2,1,0:T(8,128)S(1)} %bitcast.3, f32[2,3,8,128]{3,2,1,0:T(8,128)S(1)} %bitcast.4, f32[2,8,128]{2,1,0:T(8,128)S(1)} %copy-done.2), custom_call_target="tpu_custom_call" | custom-call | tf_op jit(solution)/shard_map/sph_step/pallas_call | solution.py:323
  35.5 0.6 %copy.10 = f32[2,8,128]{2,1,0:T(8,128)} copy(f32[2,8,128]{2,1,0:T(8,128)S(1)} %get-tuple-element.8) | data formatting | bytes 16384
  36.1 0.6 %copy.11 = f32[2,8,128,3]{2,1,3,0:T(8,128)} copy(f32[2,8,128,3]{2,1,3,0:T(8,128)S(1)} %bitcast.5) | data formatting | bytes 49152
Async XLA Ops:
  1.3 0.7 %copy-start.3 = (s32[2,8]{1,0:T(2,128)S(1)}, s32[2,8]{1,0:T(2,128)}, u32[]{:S(2)}) copy-start(s32[2,8]{1,0:T(2,128)} %counts.1) | copy-start | bytes 196
  2.0 0.7 %copy-start = (f32[2,8,128,3]{2,1,3,0:T(8,128)S(1)}, f32[2,8,128,3]{2,1,3,0:T(8,128)}, u32[]{:S(2)}) copy-start(f32[2,8,128,3]{2,1,3,0:T(8,128)} %param.5) | copy-start | bytes 73732
  2.7 0.7 %copy-start.1 = (f32[2,8,128,3]{2,1,3,0:T(8,128)S(1)}, f32[2,8,128,3]{2,1,3,0:T(8,128)}, u32[]{:S(2)}) copy-start(f32[2,8,128,3]{2,1,3,0:T(8,128)} %param.6) | copy-start | bytes 73732
  3.4 0.7 %copy-start.2 = (f32[2,8,128]{2,1,0:T(8,128)S(1)}, f32[2,8,128]{2,1,0:T(8,128)}, u32[]{:S(2)}) copy-start(f32[2,8,128]{2,1,0:T(8,128)} %mass.1) | copy-start | bytes 24580

commit v2 on v1

v2 whole, which is shorter than its diff:
```python
import functools
import math

import jax
import jax.numpy as jnp
from jax import lax
from jax.experimental import pallas as pl
from jax.experimental.pallas import tpu as pltpu
from jax.sharding import PartitionSpec as P

SMOOTHING = 0.5
KERNEL_NORM = 1.0 / (math.pi * SMOOTHING**3)
SOUND_SQ = 0.2
VISCOSITY = 0.05
SOFTENING = 0.0025
SHEAR_JUMP = 1.0

MESH = pl.DeviceIdType.MESH
F32 = jnp.float32
BF16 = jnp.bfloat16
RHO_SCALE = KERNEL_NORM * 0.25
GRAD_SCALE = KERNEL_NORM * 0.75 / (SMOOTHING * SMOOTHING)
SOFT_Q = SOFTENING / (SMOOTHING * SMOOTHING)
TINY_Q = 1e-8
SLOTS = 128
ROWS = 2
COLS = 8
WIDTH = (2, 1, 1)
DRIFT = 4
EDGE = tuple(w + DRIFT for w in WIDTH)
WINDOW = tuple(2 * e + COLS for e in EDGE)
FAR = 3
EXTRA = 4


def pieces(p):
    high = p.astype(BF16).astype(F32)
    rest = p - high
    middle = rest.astype(BF16).astype(F32)
    return high, middle, rest - middle


def zeros(n):
    return jnp.zeros((n, SLOTS), F32)


def kernel(
    ny, nx,
    counts_in, shift, pos_in, vel_in, mass_in,
    dens_out, acc_out,
    own_a, own_v, own_m,
    below_a, below_v, below_m,
    above_a, above_v, above_m,
    side_a, side_v, side_m,
    far_a, far_m,
    near, centre, far_centre, feats, mass_cols,
    g_high, g_low, e_part,
    rho_part, sums,
    counts, pos, vel, mass,
    send_sem, recv_sem, load_sem,
):
    gy, gx = lax.axis_index("gy"), lax.axis_index("gx")
    top = gy // (ny - 1)
    bottom = (ny - 1 - gy) // (ny - 1)
    half = nx // 2
    up_y, down_y = lax.rem(gy + 1, ny), lax.rem(gy + ny - 1, ny)

    def up_id(k):
        return (up_y, lax.rem(gx + half * top + k + nx, nx))

    def down_id(k):
        return (down_y, lax.rem(gx + half * bottom + k + nx, nx))

    left_id = (gy, lax.rem(gx + nx - 1, nx))
    right_id = (gy, lax.rem(gx + 1, nx))

    row_a, row_v, row_m = (below_a, above_a), (below_v, above_v), (below_m, above_m)
    barrier = pltpu.get_barrier_semaphore()
    for k in (0, -1, 1):
        pl.semaphore_signal(barrier, inc=1, device_id=up_id(k), device_id_type=MESH)
        pl.semaphore_signal(barrier, inc=1, device_id=down_id(k), device_id_type=MESH)
    pl.semaphore_signal(barrier, inc=1, device_id=left_id, device_id_type=MESH)
    pl.semaphore_signal(barrier, inc=1, device_id=right_id, device_id_type=MESH)

    loads = [
        pltpu.make_async_copy(src, dst, load_sem.at[i])
        for i, (src, dst) in enumerate(
            ((counts_in, counts), (pos_in, pos), (mass_in, mass), (vel_in, vel))
        )
    ]
    for load in loads:
        load.start()

    def copy_of(phase, slot, src, dst, device):
        return pltpu.make_async_remote_copy(
            src_ref=src,
            dst_ref=dst,
            send_sem=send_sem.at[phase, slot],
            recv_sem=recv_sem.at[phase, slot],
            device_id=device,
            device_id_type=MESH,
        )

    def spans(edge):
        return ((1, COLS - edge, edge, 0), (0, 0, COLS, edge), (-1, 0, edge, edge + COLS))

    def row_copies(phase, slot, src, dst, device):
        return [
            copy_of(phase, slot - k, src.at[pl.ds(start, count)], dst.at[pl.ds(at, count)], device(k))
            for k, start, count, at in spans(EDGE[phase % FAR])
        ]

    def up_copies(phase, own, row):
        return row_copies(phase, 1, own.at[1], row[0], up_id)

    def down_copies(phase, own, row):
        return row_copies(phase, 4, own.at[0], row[1], down_id)

    def side_copies(phase, own, side):
        w = WIDTH[phase]
        return [
            copy_of(phase, 6, own.at[:, pl.ds(COLS - w, w)], side.at[0], right_id),
            copy_of(phase, 7, own.at[:, pl.ds(0, w)], side.at[1], left_id),
        ]

    def far_copies():
        return (
            row_copies(FAR, 1, own_a.at[0], far_a, up_id),
            row_copies(FAR, 1, own_a.at[1], far_a, down_id),
        )

    def start(copies):
        for copy in copies:
            copy.start()

    def wait_row(phase, own, row, d):
        for copy in row_copies(phase, 3 * d + 1, own.at[0], row[d], lambda k: left_id):
            copy.wait_recv()

    def wait_side(phase, own, side):
        for copy in side_copies(phase, own, side):
            copy.wait_recv()

    lane = lax.broadcasted_iota(jnp.int32, (COLS, SLOTS), 1)
    column = lax.broadcasted_iota(jnp.int32, (COLS, SLOTS), 0).astype(F32)

    def valid_of(r):
        bound = jnp.concatenate([jnp.full((1, SLOTS), counts[r, c], jnp.int32) for c in range(COLS)], axis=0)
        return lane < bound

    for load in loads:
        load.wait()
    for r in range(ROWS):
        fields = [pos[r, 0], pos[r, 1], pos[r, 2], jnp.where(valid_of(r), mass[r], 0.0)]
        for f in range(4):
            for c in range(COLS):
                own_a[r, c, f : f + 1, :] = fields[f][c : c + 1, :]
        for f in range(3):
            for c in range(COLS):
                own_v[r, c, f : f + 1, :] = vel[r, f][c : c + 1, :]
        for c in range(COLS):
            own_v[r, c, 3:4, :] = zeros(1)

    def scaled(xyzw, j, row):
        row = row.astype(F32) if hasattr(row, "astype") else float(row)
        x = 2.0 * xyzw[0:1] + (2.0 * j - 10.0)
        y = 2.0 * xyzw[1:2] + (2.0 * row - 4.0)
        return x, y, 2.0 * xyzw[2:3] - 1.0

    def prepare(e, j, xyzw, row=None):
        x, y, z = scaled(xyzw, j, e if row is None else row)
        w = xyzw[3:4]
        n = x * x + y * y + z * z
        lhs = jnp.concatenate([x, y, z, n, jnp.ones((1, SLOTS), F32), w, zeros(2)], axis=0)
        high, middle, low = pieces(lhs)
        table = jnp.concatenate([high, high, high, middle, middle, low, lhs, zeros(8)], axis=0).T
        at = (j + 1) * SLOTS
        near[e, at : at + SLOTS, :] = table.astype(BF16)
        mass_cols[e, at : at + SLOTS, :] = jnp.broadcast_to(table[:, 53:54], (SLOTS, SLOTS))
        if row is None and 0 <= j < COLS + 2:
            first = jnp.concatenate([w, w * x, w * y, w * z, zeros(4)], axis=0)
            feats[e, 32:64, j * SLOTS : (j + 1) * SLOTS] = jnp.concatenate([*pieces(first), zeros(8)], axis=0).astype(BF16)

    def centre_of(xyzw, j, row):
        x, y, z = scaled(xyzw, j, row)
        n = x * x + y * y + z * z
        rhs = jnp.concatenate([-2.0 * x, -2.0 * y, -2.0 * z, jnp.ones((1, SLOTS), F32), n, zeros(3)], axis=0)
        high, middle, low = pieces(rhs)
        return jnp.concatenate([high, middle, low, high, middle, high, zeros(16)], axis=0).astype(BF16)

    def prepare_own(r, carry):
        for c in range(COLS):
            prepare(r + 1, c + 1, own_a[r, c])
            centre[r, c] = centre_of(own_a[r, c], c + 1, r + 1)
        return carry

    lax.fori_loop(0, ROWS, prepare_own, 0)
    rho_part[...] = jnp.zeros_like(rho_part)
    sums[...] = jnp.zeros_like(sums)

    pl.semaphore_wait(barrier, 8)
    sent_a = up_copies(0, own_a, row_a) + down_copies(0, own_a, row_a) + side_copies(0, own_a, side_a)
    sent_v = up_copies(1, own_v, row_v) + down_copies(1, own_v, row_v) + side_copies(1, own_v, side_v)
    sent_up, sent_down = far_copies()
    start(sent_a)
    pl.when(top == 1)(lambda: start(sent_up))
    pl.when(bottom == 1)(lambda: start(sent_down))
    start(sent_v)

    def kernel_of(cells, rhs):
        q_sq = jnp.maximum(jnp.dot(cells, rhs, preferred_element_type=F32), TINY_Q)
        inverse = lax.rsqrt(q_sq)
        q = q_sq * inverse
        u = jnp.maximum(2.0 - q, 0.0)
        s = jnp.maximum(1.0 - q, 0.0)
        u_sq = u * u
        s_sq = 4.0 * (s * s)
        return u_sq * u - s_sq * s, (s_sq - u_sq) * inverse, q_sq

    def pairs(r, a, c):
        e = r + a
        total = rho_part[r, c]
        rhs = centre[r, c]
        for b in range(3):
            at = (c + b + 1) * SLOTS
            value, slope, q_sq = kernel_of(near[e, at : at + SLOTS, :], rhs)
            soft = lax.rsqrt(q_sq + SOFT_Q)
            extra = (slope * soft) * soft
            weighted = value * mass_cols[e, at : at + SLOTS, :]
            total = total + jnp.sum(weighted.reshape(SLOTS // 8, 8, SLOTS), axis=0)
            high = slope.astype(BF16)
            span = pl.ds(b * SLOTS, SLOTS)
            g_high[r, a, c, span, :] = high
            g_low[r, a, c, span, :] = (slope - high.astype(F32)).astype(BF16)
            e_part[r, a, c, span, :] = extra.astype(BF16)
        rho_part[r, c] = total

    def reduce(r, a, c):
        e = r + a
        lanes = pl.ds(c * SLOTS, 3 * SLOTS)
        rows = feats[e, :, lanes]
        g = jnp.dot(rows, g_high[r, a, c], preferred_element_type=F32)
        g = g + jnp.dot(rows, g_low[r, a, c], preferred_element_type=F32)
        v = jnp.dot(rows[0:32], e_part[r, a, c], preferred_element_type=F32)
        sums[r, c, 0:8, :] += g[0:8] + g[8:16] + g[16:24]
        sums[r, c, 8:16, :] += g[32:40] + g[40:48] + g[48:56]
        sums[r, c, 16:24, :] += v[0:8] + v[8:16] + v[16:24]

    def own_units(work, cells):
        def body(t, carry):
            r = t // 2
            a = 1 - r + lax.rem(t, 2)
            for c in cells:
                work(r, a, c)
            return carry

        lax.fori_loop(0, 4, body, 0)

    inner, outer = tuple(range(1, COLS - 1)), (0, COLS - 1)
    own_units(pairs, inner)
    wait_side(0, own_a, side_a)
    for s in (0, 1):
        for r in range(ROWS):
            prepare(r + 1, (COLS + 1) * s, side_a[s, r, 1 - s])
    own_units(pairs, outer)

    drift = jnp.clip(shift[0] - half * COLS, -DRIFT, DRIFT)
    drifts = (bottom * drift, -top * drift)
    far_side = (bottom, top)

    def window(phase, d, j):
        return EDGE[phase] - 1 + drifts[d] + j

    def both_rows(work):
        pl.when(bottom == 1)(lambda: work(1))
        work(0)
        pl.when(bottom == 0)(lambda: work(1))

    def ghost_pairs(d):
        wait_row(0, own_a, row_a, d)
        for j in range(COLS + 2):
            prepare(3 * d, j, row_a[d][window(0, d, j)])
        for c in range(COLS):
            pairs(d, 2 * d, c)

    both_rows(ghost_pairs)

    valid = [valid_of(r) for r in range(ROWS)]
    inverse_rho = []
    for r in range(ROWS):
        rho = jnp.concatenate([jnp.sum(rho_part[r, c], axis=0, keepdims=True) for c in range(COLS)], axis=0) * RHO_SCALE
        dens_out[r] = jnp.where(valid[r], rho, 0.0)
        inv = 1.0 / jnp.where(valid[r], rho, 1.0)
        inverse_rho.append(inv)
        ratio = jnp.where(valid[r], mass[r], 0.0) * inv
        for c in range(COLS):
            own_m[r, c] = ratio[c : c + 1, :]
    sent_m = up_copies(2, own_m, row_m), down_copies(2, own_m, row_m), side_copies(2, own_m, side_m)
    pl.when(top == 0)(lambda: start(sent_m[0]))
    pl.when(bottom == 0)(lambda: start(sent_m[1]))
    start(sent_m[2])

    def far_tables(d):
        for copy in row_copies(FAR, 1, own_a.at[0], far_a, lambda k: left_id):
            copy.wait_recv()
        for j in range(-1, COLS + 3):
            prepare(EXTRA, j, far_a[window(0, d, j)], row=5 * d - 1)
        for s in (0, 1):
            j = (COLS + 3) * s - 1
            prepare(3 * d, j, row_a[d][window(0, d, j)])
            prepare(d + 1, j, side_a[s, d, s])
        for j in range(COLS + 2):
            far_centre[j] = centre_of(row_a[d][window(0, d, j)], j, 3 * d)

    def far_density(d):
        def body(t, carry):
            for i in range(5):
                j = 5 * t + i
                total = zeros(8)
                rhs = far_centre[j]
                for e in (d + 1, 3 * d, EXTRA):
                    for b in range(3):
                        at = pl.multiple_of((j + b) * SLOTS, SLOTS)
                        value, _, _ = kernel_of(near[e, pl.ds(at, SLOTS), :], rhs)
                        weighted = value * mass_cols[e, pl.ds(at, SLOTS), :]
                        total = total + jnp.sum(weighted.reshape(SLOTS // 8, 8, SLOTS), axis=0)
                far_m[j] = jnp.sum(total, axis=0, keepdims=True) * RHO_SCALE
            return carry

        lax.fori_loop(0, 2, body, 0)

    pl.when(bottom == 1)(lambda: far_tables(0))
    pl.when(top == 1)(lambda: far_tables(1))
    pl.when(bottom + top == 1)(lambda: far_density(top))

    def second(e, j, xyzw, v, ratio, jump):
        x, y, z = scaled(xyzw, j, e)
        block = jnp.concatenate(
            [ratio, ratio * x, ratio * y, ratio * z, ratio * (v[0:1] + jump), ratio * v[1:2], ratio * v[2:3], zeros(1)],
            axis=0,
        )
        feats[e, 0:32, j * SLOTS : (j + 1) * SLOTS] = jnp.concatenate([*pieces(block), zeros(8)], axis=0).astype(BF16)

    def second_own(r, carry):
        for c in range(COLS):
            second(r + 1, c + 1, own_a[r, c], own_v[r, c], own_m[r, c], 0.0)
        return carry

    lax.fori_loop(0, ROWS, second_own, 0)
    own_units(reduce, inner)
    wait_side(1, own_v, side_v)
    wait_side(2, own_m, side_m)
    for s in (0, 1):
        for r in range(ROWS):
            second(r + 1, (COLS + 1) * s, side_a[s, r, 1 - s], side_v[s, r, 0], side_m[s, r, 0], 0.0)
    own_units(reduce, outer)

    jumps = (-(bottom.astype(F32)) * SHEAR_JUMP, top.astype(F32) * SHEAR_JUMP)

    def ghost_reduce(d):
        wait_row(1, own_v, row_v, d)
        pl.when(far_side[d] == 0)(lambda: wait_row(2, own_m, row_m, d))
        for j in range(COLS + 2):
            xyzw = row_a[d][window(0, d, j)]
            w = xyzw[3:4]
            far_ratio = w / jnp.where(w > 0.0, far_m[j], 1.0)
            ratio = jnp.where(far_side[d] == 1, far_ratio, row_m[d][window(2, d, j)])
            second(3 * d, j, xyzw, row_v[d][window(1, d, j)], ratio, jumps[d])
        for c in range(COLS):
            reduce(d, 2 * d, c)

    both_rows(ghost_reduce)

    for r in range(ROWS):
        def row_of(k):
            return jnp.concatenate([sums[r, c, k : k + 1, :] for c in range(COLS)], axis=0)

        block = [
            2.0 * pos[r, 0] + (2.0 * column - 8.0),
            2.0 * pos[r, 1] + (2.0 * r - 2.0),
            2.0 * pos[r, 2] - 1.0,
        ]
        inv = inverse_rho[r]
        ratio_sum, mass_sum = row_of(0), row_of(8)
        visc_sum = ratio_sum - SOFT_Q * row_of(16)
        for f in range(3):
            far = block[f] * ratio_sum - row_of(1 + f)
            near_part = block[f] * mass_sum - row_of(9 + f)
            drag = vel[r, f] * visc_sum - (row_of(4 + f) - SOFT_Q * row_of(20 + f))
            total = (-0.5 * SOUND_SQ * GRAD_SCALE) * (inv * near_part + far) + (2.0 * VISCOSITY * GRAD_SCALE) * (inv * drag)
            acc_out[r, f] = jnp.where(valid[r], total, 0.0)

    def drain(copies):
        for copy in copies:
            copy.wait_send()

    drain(sent_a + sent_v + sent_m[2])
    pl.when(top == 1)(lambda: drain(sent_up))
    pl.when(top == 0)(lambda: drain(sent_m[0]))
    pl.when(bottom == 1)(lambda: drain(sent_down))
    pl.when(bottom == 0)(lambda: drain(sent_m[1]))


def local(ny, nx, position, velocity, particle_mass, cell_counts, shear_shift):
    pos = jnp.transpose(position, (0, 3, 1, 2))
    vel = jnp.transpose(velocity, (0, 3, 1, 2))
    vmem = pl.BlockSpec(memory_space=pltpu.VMEM)
    hbm = pl.BlockSpec(memory_space=pltpu.HBM)
    in_hbm = functools.partial(pltpu.with_memory_space_constraint, memory_space=pltpu.HBM)
    table = (ROWS, 3, COLS, 3 * SLOTS, SLOTS)
    density, accel = pl.pallas_call(
        functools.partial(kernel, ny, nx),
        out_shape=(
            jax.ShapeDtypeStruct((ROWS, COLS, SLOTS), F32),
            jax.ShapeDtypeStruct((ROWS, 3, COLS, SLOTS), F32),
        ),
        in_specs=[hbm, pl.BlockSpec(memory_space=pltpu.SMEM), hbm, hbm, hbm],
        out_specs=(vmem, vmem),
        scratch_shapes=[
            pltpu.VMEM((ROWS, COLS, 4, SLOTS), F32),
            pltpu.VMEM((ROWS, COLS, 4, SLOTS), F32),
            pltpu.VMEM((ROWS, COLS, 1, SLOTS), F32),
            *(pltpu.VMEM((w, f, SLOTS), F32) for _ in range(2) for w, f in zip(WINDOW, (4, 4, 1))),
            *(pltpu.VMEM((2, ROWS, w, f, SLOTS), F32) for w, f in zip(WIDTH, (4, 4, 1))),
            pltpu.VMEM((WINDOW[0], 4, SLOTS), F32),
            pltpu.VMEM((COLS + 2, 1, SLOTS), F32),
            pltpu.VMEM((ROWS + 3, (COLS + 4) * SLOTS, 64), BF16),
            pltpu.VMEM((ROWS, COLS, 64, SLOTS), BF16),
            pltpu.VMEM((COLS + 2, 64, SLOTS), BF16),
            pltpu.VMEM((ROWS + 2, 64, (COLS + 2) * SLOTS), BF16),
            pltpu.VMEM((ROWS + 3, (COLS + 4) * SLOTS, SLOTS), F32),
            pltpu.VMEM(table, BF16),
            pltpu.VMEM(table, BF16),
            pltpu.VMEM(table, BF16),
            pltpu.VMEM((ROWS, COLS, 8, SLOTS), F32),
            pltpu.VMEM((ROWS, COLS, 24, SLOTS), F32),
            pltpu.SMEM((ROWS, COLS), jnp.int32),
            pltpu.VMEM((ROWS, 3, COLS, SLOTS), F32),
            pltpu.VMEM((ROWS, 3, COLS, SLOTS), F32),
            pltpu.VMEM((ROWS, COLS, SLOTS), F32),
            pltpu.SemaphoreType.DMA((4, 8)),
            pltpu.SemaphoreType.DMA((4, 8)),
            pltpu.SemaphoreType.DMA((4,)),
        ],
        compiler_params=pltpu.CompilerParams(
            collective_id=0, has_side_effects=True, vmem_limit_bytes=48 * 1024 * 1024
        ),
        name="sph_step",
    )(in_hbm(cell_counts), shear_shift, in_hbm(pos), in_hbm(vel), in_hbm(particle_mass))
    return density, jnp.transpose(accel, (0, 2, 3, 1))


def solution(mesh):
    placed = (
        P("gy", "gx", None, None),
        P("gy", "gx", None, None),
        P("gy", "gx", None),
        P("gy", "gx"),
        P(),
    )
    return jax.shard_map(
        functools.partial(local, mesh.shape["gy"], mesh.shape["gx"]),
        mesh=mesh,
        in_specs=placed,
        out_specs=(P("gy", "gx", None), P("gy", "gx", None, None)),
        check_vma=False,
    )
```

time: 37 us -> 35.1 us (0.949)
  the two profiles are of different devices: /device:TPU:7 before, /device:TPU:24 now
where the time goes in v2:
time: 35.1 us; the launch traced here: 34.9 us
  Pallas kernels  32.4 us (92%)
  between operations  1.29 us (4%)
  local copies, waits for them, and re-layouts  1.21 us (3%)
    pallas_call x1, Pallas kernels, local(): pl.pallas_call(functools.partial(kernel, ny, nx), out_shape=(jax.ShapeDty...  32.4 us
    unnamed x2, local copies, waits for them, and re-layouts  1.21 us

profile of v2, /device:TPU:24, one launch (start us, length us, event | category | flops | bytes accessed | tf_op | source)
XLA Modules:
  0.0 34.9 jit_solution(10536866026156238652)
XLA Ops:
  1.3 32.4 %sph_step.1 = (f32[2,8,128]{2,1,0:T(8,128)S(1)}, f32[2,3,8,128]{3,2,1,0:T(8,128)S(1)}) custom-call(s32[2,8]{1,0:T(2,128)} %counts_in.1, s32[1]{0:T(128)S(6)} %copy.9.shift, f32[2,3,8,128]{3,2,1,0:T(8,128)} %bitcast.4, f32[2,3,8,128]{3,2,1,0:T(8,128)} %bitcast.5, f32[2,8,128]{2,1,0:T(8,128)} %mass_in.1), custom_call_target="tpu_custom_call" | custom-call | tf_op jit(solution)/shard_map/sph_step/pallas_call | solution.py:411
  33.7 0.6 %copy.10 = f32[2,8,128]{2,1,0:T(8,128)} copy(f32[2,8,128]{2,1,0:T(8,128)S(1)} %get-tuple-element.8) | data formatting | bytes 16384
  34.3 0.6 %copy.11 = f32[2,8,128,3]{2,1,3,0:T(8,128)} copy(f32[2,8,128,3]{2,1,3,0:T(8,128)S(1)} %bitcast.3) | data formatting | bytes 49152

commit v3 on v2

--- a/solution.py
+++ b/solution.py
@@ -141,6 +141,8 @@
         for copy in side_copies(phase, own, side):
             copy.wait_recv()
 
+    spot = lax.broadcasted_iota(jnp.int32, (64, SLOTS), 0)
+    pick_mass = ((spot == 5) | (spot == 29) | (spot == 45)).astype(F32).astype(BF16)
     lane = lax.broadcasted_iota(jnp.int32, (COLS, SLOTS), 1)
     column = lax.broadcasted_iota(jnp.int32, (COLS, SLOTS), 0).astype(F32)
 
@@ -173,10 +175,10 @@
         n = x * x + y * y + z * z
         lhs = jnp.concatenate([x, y, z, n, jnp.ones((1, SLOTS), F32), w, zeros(2)], axis=0)
         high, middle, low = pieces(lhs)
-        table = jnp.concatenate([high, high, high, middle, middle, low, lhs, zeros(8)], axis=0).T
+        table = jnp.concatenate([high, high, high, middle, middle, low, zeros(16)], axis=0).T
         at = (j + 1) * SLOTS
         near[e, at : at + SLOTS, :] = table.astype(BF16)
-        mass_cols[e, at : at + SLOTS, :] = jnp.broadcast_to(table[:, 53:54], (SLOTS, SLOTS))
+        mass_cols[e, at : at + SLOTS, :] = jnp.dot(table.astype(BF16), pick_mass, preferred_element_type=F32)
         if row is None and 0 <= j < COLS + 2:
             first = jnp.concatenate([w, w * x, w * y, w * z, zeros(4)], axis=0)
             feats[e, 32:64, j * SLOTS : (j + 1) * SLOTS] = jnp.concatenate([*pieces(first), zeros(8)], axis=0).astype(BF16)
@@ -194,18 +196,22 @@
             centre[r, c] = centre_of(own_a[r, c], c + 1, r + 1)
         return carry
 
+    sent_a = up_copies(0, own_a, row_a) + down_copies(0, own_a, row_a) + side_copies(0, own_a, side_a)
+    sent_v = up_copies(1, own_v, row_v) + down_copies(1, own_v, row_v) + side_copies(1, own_v, side_v)
+    sent_up, sent_down = far_copies()
+
+    def exchange():
+        pl.semaphore_wait(barrier, 8)
+        start(sent_a)
+        pl.when(top == 1)(lambda: start(sent_up))
+        pl.when(bottom == 1)(lambda: start(sent_down))
+        start(sent_v)
+
+    patient = (top + bottom) * (1 - gx // half)
+    pl.when(patient == 0)(exchange)
     lax.fori_loop(0, ROWS, prepare_own, 0)
     rho_part[...] = jnp.zeros_like(rho_part)
     sums[...] = jnp.zeros_like(sums)
-
-    pl.semaphore_wait(barrier, 8)
-    sent_a = up_copies(0, own_a, row_a) + down_copies(0, own_a, row_a) + side_copies(0, own_a, side_a)
-    sent_v = up_copies(1, own_v, row_v) + down_copies(1, own_v, row_v) + side_copies(1, own_v, side_v)
-    sent_up, sent_down = far_copies()
-    start(sent_a)
-    pl.when(top == 1)(lambda: start(sent_up))
-    pl.when(bottom == 1)(lambda: start(sent_down))
-    start(sent_v)
 
     def kernel_of(cells, rhs):
         q_sq = jnp.maximum(jnp.dot(cells, rhs, preferred_element_type=F32), TINY_Q)
@@ -258,32 +264,37 @@
 
     inner, outer = tuple(range(1, COLS - 1)), (0, COLS - 1)
     own_units(pairs, inner)
+    drift = jnp.clip(shift[0] - half * COLS, -DRIFT, DRIFT)
+    drifts = (bottom * drift, -top * drift)
+    far_side = (bottom, top)
+
+    def window(phase, d, j):
+        return EDGE[phase] - 1 + drifts[d] + j
+
+    def near_row(work):
+        pl.when(bottom == 1)(lambda: work(1))
+        pl.when(bottom == 0)(lambda: work(0))
+
+    def last_row(work):
+        pl.when(bottom == 1)(lambda: work(0))
+        pl.when(bottom == 0)(lambda: work(1))
+
+    def ghost_pairs(d):
+        wait_row(0, own_a, row_a, d)
+        for j in range(COLS + 2):
+            prepare(3 * d, j, row_a[d][window(0, d, j)])
+        for c in range(COLS):
+            pairs(d, 2 * d, c)
+
+    near_row(ghost_pairs)
+    pl.when(patient == 1)(exchange)
     wait_side(0, own_a, side_a)
     for s in (0, 1):
         for r in range(ROWS):
             prepare(r + 1, (COLS + 1) * s, side_a[s, r, 1 - s])
     own_units(pairs, outer)
 
-    drift = jnp.clip(shift[0] - half * COLS, -DRIFT, DRIFT)
-    drifts = (bottom * drift, -top * drift)
-    far_side = (bottom, top)
-
-    def window(phase, d, j):
-        return EDGE[phase] - 1 + drifts[d] + j
-
-    def both_rows(work):
-        pl.when(bottom == 1)(lambda: work(1))
-        work(0)
-        pl.when(bottom == 0)(lambda: work(1))
-
-    def ghost_pairs(d):
-        wait_row(0, own_a, row_a, d)
-        for j in range(COLS + 2):
-            prepare(3 * d, j, row_a[d][window(0, d, j)])
-        for c in range(COLS):
-            pairs(d, 2 * d, c)
-
-    both_rows(ghost_pairs)
+    last_row(ghost_pairs)
 
     valid = [valid_of(r) for r in range(ROWS)]
     inverse_rho = []
@@ -318,20 +329,19 @@
                 j = 5 * t + i
                 total = zeros(8)
                 rhs = far_centre[j]
-                for e in (d + 1, 3 * d, EXTRA):
+                for n, e in enumerate((d + 1, 3 * d, EXTRA)):
                     for b in range(3):
                         at = pl.multiple_of((j + b) * SLOTS, SLOTS)
                         value, _, _ = kernel_of(near[e, pl.ds(at, SLOTS), :], rhs)
                         weighted = value * mass_cols[e, pl.ds(at, SLOTS), :]
                         total = total + jnp.sum(weighted.reshape(SLOTS // 8, 8, SLOTS), axis=0)
+                    turn = 3 * i + n
+                    if turn < 2 * len(inner):
+                        reduce(t, 1 - t + turn // len(inner), inner[turn % len(inner)])
                 far_m[j] = jnp.sum(total, axis=0, keepdims=True) * RHO_SCALE
             return carry
 
         lax.fori_loop(0, 2, body, 0)
-
-    pl.when(bottom == 1)(lambda: far_tables(0))
-    pl.when(top == 1)(lambda: far_tables(1))
-    pl.when(bottom + top == 1)(lambda: far_density(top))
 
     def second(e, j, xyzw, v, ratio, jump):
         x, y, z = scaled(xyzw, j, e)
@@ -347,7 +357,10 @@
         return carry
 
     lax.fori_loop(0, ROWS, second_own, 0)
-    own_units(reduce, inner)
+    pl.when(bottom == 1)(lambda: far_tables(0))
+    pl.when(top == 1)(lambda: far_tables(1))
+    pl.when(bottom + top == 1)(lambda: far_density(top))
+    pl.when(bottom + top == 0)(lambda: own_units(reduce, inner))
     wait_side(1, own_v, side_v)
     wait_side(2, own_m, side_m)
     for s in (0, 1):
@@ -369,7 +382,8 @@
         for c in range(COLS):
             reduce(d, 2 * d, c)
 
-    both_rows(ghost_reduce)
+    near_row(ghost_reduce)
+    last_row(ghost_reduce)
 
     for r in range(ROWS):
         def row_of(k):

time: 35.1 us -> 37.9 us (1.080)
  the two profiles are of different devices: /device:TPU:24 before, /device:TPU:1 now
where the time goes in v3:
time: 37.9 us; the launch traced here: 37.7 us
  Pallas kernels  35.2 us (93%)
  between operations  1.29 us (3%)
  local copies, waits for them, and re-layouts  1.21 us (3%)
    pallas_call x1, Pallas kernels, local(): pl.pallas_call(functools.partial(kernel, ny, nx), out_shape=(jax.ShapeDty...  35.2 us
    unnamed x2, local copies, waits for them, and re-layouts  1.21 us

profile of v3, /device:TPU:1, one launch (start us, length us, event | category | flops | bytes accessed | tf_op | source)
XLA Modules:
  0.0 37.7 jit_solution(17939786621232843227)
XLA Ops:
  1.3 35.2 %sph_step.1 = (f32[2,8,128]{2,1,0:T(8,128)S(1)}, f32[2,3,8,128]{3,2,1,0:T(8,128)S(1)}) custom-call(s32[2,8]{1,0:T(2,128)} %counts_in.1, s32[1]{0:T(128)S(6)} %copy.9.shift, f32[2,3,8,128]{3,2,1,0:T(8,128)} %bitcast.4, f32[2,3,8,128]{3,2,1,0:T(8,128)} %bitcast.5, f32[2,8,128]{2,1,0:T(8,128)} %mass_in.1), custom_call_target="tpu_custom_call" | custom-call | tf_op jit(solution)/shard_map/sph_step/pallas_call | solution.py:425
  36.5 0.6 %copy.10 = f32[2,8,128]{2,1,0:T(8,128)} copy(f32[2,8,128]{2,1,0:T(8,128)S(1)} %get-tuple-element.8) | data formatting | bytes 16384
  37.1 0.6 %copy.11 = f32[2,8,128,3]{2,1,3,0:T(8,128)} copy(f32[2,8,128,3]{2,1,3,0:T(8,128)S(1)} %bitcast.3) | data formatting | bytes 49152

commit v4 on v3

--- a/solution.py
+++ b/solution.py
@@ -207,7 +207,8 @@
         pl.when(bottom == 1)(lambda: start(sent_down))
         start(sent_v)
 
-    patient = (top + bottom) * (1 - gx // half)
+    first = (nx - gx) // nx
+    patient = jnp.maximum((top + bottom) * (1 - gx // half), first)
     pl.when(patient == 0)(exchange)
     lax.fori_loop(0, ROWS, prepare_own, 0)
     rho_part[...] = jnp.zeros_like(rho_part)
@@ -286,7 +287,6 @@
         for c in range(COLS):
             pairs(d, 2 * d, c)
 
-    near_row(ghost_pairs)
     pl.when(patient == 1)(exchange)
     wait_side(0, own_a, side_a)
     for s in (0, 1):
@@ -294,6 +294,7 @@
             prepare(r + 1, (COLS + 1) * s, side_a[s, r, 1 - s])
     own_units(pairs, outer)
 
+    near_row(ghost_pairs)
     last_row(ghost_pairs)
 
     valid = [valid_of(r) for r in range(ROWS)]

time: 37.9 us -> 33.9 us (0.89)
  Pallas kernels: 35.2 us -> 31.2 us
    pallas_call x1, Pallas kernels: 35.2 us -> 31.2 us  [local(): pl.pallas_call(functools.partial(kernel, ny, nx), out_shape=(jax.ShapeDty...]
where the time goes in v4:
time: 33.9 us; the launch traced here: 33.7 us
  Pallas kernels  31.2 us (92%)
  between operations  1.29 us (4%)
  local copies, waits for them, and re-layouts  1.21 us (4%)
    pallas_call x1, Pallas kernels, local(): pl.pallas_call(functools.partial(kernel, ny, nx), out_shape=(jax.ShapeDty...  31.2 us
    unnamed x2, local copies, waits for them, and re-layouts  1.21 us

profile of v4, /device:TPU:1, one launch (start us, length us, event | category | flops | bytes accessed | tf_op | source)
XLA Modules:
  0.0 33.7 jit_solution(13042890149424281752)
XLA Ops:
  1.3 31.2 %sph_step.1 = (f32[2,8,128]{2,1,0:T(8,128)S(1)}, f32[2,3,8,128]{3,2,1,0:T(8,128)S(1)}) custom-call(s32[2,8]{1,0:T(2,128)} %counts_in.1, s32[1]{0:T(128)S(6)} %copy.9.shift, f32[2,3,8,128]{3,2,1,0:T(8,128)} %bitcast.4, f32[2,3,8,128]{3,2,1,0:T(8,128)} %bitcast.5, f32[2,8,128]{2,1,0:T(8,128)} %mass_in.1), custom_call_target="tpu_custom_call" | custom-call | tf_op jit(solution)/shard_map/sph_step/pallas_call | solution.py:426
  32.5 0.6 %copy.10 = f32[2,8,128]{2,1,0:T(8,128)} copy(f32[2,8,128]{2,1,0:T(8,128)S(1)} %get-tuple-element.8) | data formatting | bytes 16384
  33.1 0.6 %copy.11 = f32[2,8,128,3]{2,1,3,0:T(8,128)} copy(f32[2,8,128,3]{2,1,3,0:T(8,128)S(1)} %bitcast.3) | data formatting | bytes 49152

commit v5 on v4

--- a/solution.py
+++ b/solution.py
@@ -27,7 +27,7 @@
 COLS = 8
 WIDTH = (2, 1, 1)
 DRIFT = 4
-EDGE = tuple(w + DRIFT for w in WIDTH)
+EDGE = (WIDTH[0] + DRIFT, WIDTH[1] + DRIFT, 1)
 WINDOW = tuple(2 * e + COLS for e in EDGE)
 FAR = 3
 EXTRA = 4
@@ -102,7 +102,7 @@
         )
 
     def spans(edge):
-        return ((1, COLS - edge, edge, 0), (0, 0, COLS, edge), (-1, 0, edge, edge + COLS))
+        return ((0, 0, COLS, edge), (1, COLS - edge, edge, 0), (-1, 0, edge, edge + COLS))
 
     def row_copies(phase, slot, src, dst, device):
         return [
@@ -280,11 +280,15 @@
         pl.when(bottom == 1)(lambda: work(0))
         pl.when(bottom == 0)(lambda: work(1))
 
-    def ghost_pairs(d):
+    def ghost_first(d):
         wait_row(0, own_a, row_a, d)
         for j in range(COLS + 2):
             prepare(3 * d, j, row_a[d][window(0, d, j)])
-        for c in range(COLS):
+        for c in outer:
+            pairs(d, 2 * d, c)
+
+    def ghost_rest(d):
+        for c in inner:
             pairs(d, 2 * d, c)
 
     pl.when(patient == 1)(exchange)
@@ -294,8 +298,25 @@
             prepare(r + 1, (COLS + 1) * s, side_a[s, r, 1 - s])
     own_units(pairs, outer)
 
-    near_row(ghost_pairs)
-    last_row(ghost_pairs)
+    edge = top + bottom
+    near_row(ghost_first)
+    pl.when(edge == 1)(lambda: ghost_rest(bottom))
+    last_row(ghost_first)
+
+    sent_m = up_copies(2, own_m, row_m), down_copies(2, own_m, row_m), side_copies(2, own_m, side_m)
+    for r in range(ROWS):
+        for c in outer:
+            rho = jnp.sum(rho_part[r, c], axis=0, keepdims=True) * RHO_SCALE
+            own_m[r, c] = own_a[r, c][3:4] / jnp.where(lane[0:1] < counts[r, c], rho, 1.0)
+    start(sent_m[2])
+    pl.when(top == 0)(lambda: start(sent_m[0][1:]))
+    pl.when(bottom == 0)(lambda: start(sent_m[1][1:]))
+
+    def rest(t, carry):
+        ghost_rest(edge * top + (1 - edge) * t)
+        return carry
+
+    lax.fori_loop(edge, 2, rest, 0)
 
     valid = [valid_of(r) for r in range(ROWS)]
     inverse_rho = []
@@ -305,12 +326,10 @@
         inv = 1.0 / jnp.where(valid[r], rho, 1.0)
         inverse_rho.append(inv)
         ratio = jnp.where(valid[r], mass[r], 0.0) * inv
-        for c in range(COLS):
+        for c in inner:
             own_m[r, c] = ratio[c : c + 1, :]
-    sent_m = up_copies(2, own_m, row_m), down_copies(2, own_m, row_m), side_copies(2, own_m, side_m)
-    pl.when(top == 0)(lambda: start(sent_m[0]))
-    pl.when(bottom == 0)(lambda: start(sent_m[1]))
-    start(sent_m[2])
+    pl.when(top == 0)(lambda: start(sent_m[0][:1]))
+    pl.when(bottom == 0)(lambda: start(sent_m[1][:1]))
 
     def far_tables(d):
         for copy in row_copies(FAR, 1, own_a.at[0], far_a, lambda k: left_id):
@@ -360,8 +379,8 @@
     lax.fori_loop(0, ROWS, second_own, 0)
     pl.when(bottom == 1)(lambda: far_tables(0))
     pl.when(top == 1)(lambda: far_tables(1))
-    pl.when(bottom + top == 1)(lambda: far_density(top))
-    pl.when(bottom + top == 0)(lambda: own_units(reduce, inner))
+    pl.when(edge == 1)(lambda: far_density(top))
+    pl.when(edge == 0)(lambda: own_units(reduce, inner))
     wait_side(1, own_v, side_v)
     wait_side(2, own_m, side_m)
     for s in (0, 1):
@@ -378,7 +397,7 @@
             xyzw = row_a[d][window(0, d, j)]
             w = xyzw[3:4]
             far_ratio = w / jnp.where(w > 0.0, far_m[j], 1.0)
-            ratio = jnp.where(far_side[d] == 1, far_ratio, row_m[d][window(2, d, j)])
+            ratio = jnp.where(far_side[d] == 1, far_ratio, row_m[d][j])
             second(3 * d, j, xyzw, row_v[d][window(1, d, j)], ratio, jumps[d])
         for c in range(COLS):
             reduce(d, 2 * d, c)

time: 33.9 us -> 32.8 us (0.968)
  the two profiles are of different devices: /device:TPU:1 before, /device:TPU:16 now
where the time goes in v5:
time: 32.8 us; the launch traced here: 32.6 us
  Pallas kernels  30.1 us (92%)
  between operations  1.29 us (4%)
  local copies, waits for them, and re-layouts  1.21 us (4%)
    pallas_call x1, Pallas kernels, local(): pl.pallas_call(functools.partial(kernel, ny, nx), out_shape=(jax.ShapeDty...  30.1 us
    unnamed x2, local copies, waits for them, and re-layouts  1.21 us

profile of v5, /device:TPU:16, one launch (start us, length us, event | category | flops | bytes accessed | tf_op | source)
XLA Modules:
  0.0 32.6 jit_solution(10686410608334183808)
XLA Ops:
  1.3 30.1 %sph_step.1 = (f32[2,8,128]{2,1,0:T(8,128)S(1)}, f32[2,3,8,128]{3,2,1,0:T(8,128)S(1)}) custom-call(s32[2,8]{1,0:T(2,128)} %counts_in.1, s32[1]{0:T(128)S(6)} %copy.9.shift, f32[2,3,8,128]{3,2,1,0:T(8,128)} %bitcast.4, f32[2,3,8,128]{3,2,1,0:T(8,128)} %bitcast.5, f32[2,8,128]{2,1,0:T(8,128)} %mass_in.1), custom_call_target="tpu_custom_call" | custom-call | tf_op jit(solution)/shard_map/sph_step/pallas_call | solution.py:445
  31.4 0.6 %copy.10 = f32[2,8,128]{2,1,0:T(8,128)} copy(f32[2,8,128]{2,1,0:T(8,128)S(1)} %get-tuple-element.8) | data formatting | bytes 16384
  32.0 0.6 %copy.11 = f32[2,8,128,3]{2,1,3,0:T(8,128)} copy(f32[2,8,128,3]{2,1,3,0:T(8,128)S(1)} %bitcast.3) | data formatting | bytes 49152

commit v6 on v5

--- a/solution.py
+++ b/solution.py
@@ -292,15 +292,15 @@
             pairs(d, 2 * d, c)
 
     pl.when(patient == 1)(exchange)
+
+    edge = top + bottom
+    near_row(ghost_first)
+    pl.when(edge == 1)(lambda: ghost_rest(bottom))
     wait_side(0, own_a, side_a)
     for s in (0, 1):
         for r in range(ROWS):
             prepare(r + 1, (COLS + 1) * s, side_a[s, r, 1 - s])
     own_units(pairs, outer)
-
-    edge = top + bottom
-    near_row(ghost_first)
-    pl.when(edge == 1)(lambda: ghost_rest(bottom))
     last_row(ghost_first)
 
     sent_m = up_copies(2, own_m, row_m), down_copies(2, own_m, row_m), side_copies(2, own_m, side_m)
@@ -433,6 +433,17 @@
     pl.when(top == 0)(lambda: drain(sent_m[0]))
     pl.when(bottom == 1)(lambda: drain(sent_down))
     pl.when(bottom == 0)(lambda: drain(sent_m[1]))
+
+
+def put_out(density, accel, density_out, accel_out, sem):
+    copies = [
+        pltpu.make_async_copy(accel, accel_out, sem.at[0]),
+        pltpu.make_async_copy(density, density_out, sem.at[1]),
+    ]
+    for copy in copies:
+        copy.start()
+    for copy in copies:
+        copy.wait()
 
 
 def local(ny, nx, position, velocity, particle_mass, cell_counts, shear_shift):
@@ -481,6 +492,18 @@
         ),
         name="sph_step",
     )(in_hbm(cell_counts), shear_shift, in_hbm(pos), in_hbm(vel), in_hbm(particle_mass))
+    density, accel = pl.pallas_call(
+        put_out,
+        out_shape=(
+            jax.ShapeDtypeStruct((ROWS, COLS, SLOTS), F32),
+            jax.ShapeDtypeStruct((ROWS, 3, COLS, SLOTS), F32),
+        ),
+        in_specs=[vmem, vmem],
+        out_specs=(hbm, hbm),
+        scratch_shapes=[pltpu.SemaphoreType.DMA((2,))],
+        compiler_params=pltpu.CompilerParams(vmem_limit_bytes=1024 * 1024),
+        name="put_out",
+    )(density, accel)
     return density, jnp.transpose(accel, (0, 2, 3, 1))
 
 

time: 32.8 us -> 31.5 us (0.960)
  the two profiles are of different devices: /device:TPU:16 before, /device:TPU:7 now
where the time goes in v6:
time: 31.5 us; the launch traced here: 31.2 us
  Pallas kernels  29.9 us (95%)
  between operations  1.29 us (4%)
    pallas_call x1, Pallas kernels, local(): pl.pallas_call(functools.partial(kernel, ny, nx), out_shape=(jax.ShapeDty...  29.3 us

profile of v6, /device:TPU:7, one launch (start us, length us, event | category | flops | bytes accessed | tf_op | source)
XLA Modules:
  0.0 31.2 jit_solution(9930471337350025790)
XLA Ops:
  1.3 29.3 %sph_step.1 = (f32[2,8,128]{2,1,0:T(8,128)S(1)}, f32[2,3,8,128]{3,2,1,0:T(8,128)S(1)}) custom-call(s32[2,8]{1,0:T(2,128)} %counts_in.1, s32[1]{0:T(128)S(6)} %copy.7.shift, f32[2,3,8,128]{3,2,1,0:T(8,128)} %bitcast.3, f32[2,3,8,128]{3,2,1,0:T(8,128)} %bitcast.4, f32[2,8,128]{2,1,0:T(8,128)} %mass_in.1), custom_call_target="tpu_custom_call" | custom-call | tf_op jit(solution)/shard_map/sph_step/pallas_call | solution.py:456
  30.6 0.6 %put_out.1 = (f32[2,8,128]{2,1,0:T(8,128)}, f32[2,3,8,128]{3,2,1,0:T(8,128)}) custom-call(f32[2,8,128]{2,1,0:T(8,128)S(1)} %get-tuple-element.6.density, f32[2,3,8,128]{3,2,1,0:T(8,128)S(1)} %get-tuple-element.7.accel), custom_call_target="tpu_custom_call" | custom-call | tf_op jit(solution)/shard_map/put_out/pallas_call | solution.py:495

commit v7 on v6

--- a/solution.py
+++ b/solution.py
@@ -133,8 +133,8 @@
         for copy in copies:
             copy.start()
 
-    def wait_row(phase, own, row, d):
-        for copy in row_copies(phase, 3 * d + 1, own.at[0], row[d], lambda k: left_id):
+    def wait_row(phase, own, row, d, blocks=slice(None)):
+        for copy in row_copies(phase, 3 * d + 1, own.at[0], row[d], lambda k: left_id)[blocks]:
             copy.wait_recv()
 
     def wait_side(phase, own, side):
@@ -381,29 +381,32 @@
     pl.when(top == 1)(lambda: far_tables(1))
     pl.when(edge == 1)(lambda: far_density(top))
     pl.when(edge == 0)(lambda: own_units(reduce, inner))
+    jumps = (-(bottom.astype(F32)) * SHEAR_JUMP, top.astype(F32) * SHEAR_JUMP)
+
+    def ghost_second(d, blocks, cells):
+        pl.when(far_side[d] == 0)(lambda: wait_row(2, own_m, row_m, d, blocks))
+        for j in cells:
+            xyzw = row_a[d][window(0, d, j)]
+            w = xyzw[3:4]
+            far_ratio = w / jnp.where(w > 0.0, far_m[j], 1.0)
+            ratio = jnp.where(far_side[d] == 1, far_ratio, row_m[d][j])
+            second(3 * d, j, xyzw, row_v[d][window(1, d, j)], ratio, jumps[d])
+
+    for d in (0, 1):
+        wait_row(1, own_v, row_v, d)
+        ghost_second(d, slice(0, 1), range(1, COLS + 1))
+        for c in inner:
+            reduce(d, 2 * d, c)
     wait_side(1, own_v, side_v)
     wait_side(2, own_m, side_m)
     for s in (0, 1):
         for r in range(ROWS):
             second(r + 1, (COLS + 1) * s, side_a[s, r, 1 - s], side_v[s, r, 0], side_m[s, r, 0], 0.0)
     own_units(reduce, outer)
-
-    jumps = (-(bottom.astype(F32)) * SHEAR_JUMP, top.astype(F32) * SHEAR_JUMP)
-
-    def ghost_reduce(d):
-        wait_row(1, own_v, row_v, d)
-        pl.when(far_side[d] == 0)(lambda: wait_row(2, own_m, row_m, d))
-        for j in range(COLS + 2):
-            xyzw = row_a[d][window(0, d, j)]
-            w = xyzw[3:4]
-            far_ratio = w / jnp.where(w > 0.0, far_m[j], 1.0)
-            ratio = jnp.where(far_side[d] == 1, far_ratio, row_m[d][j])
-            second(3 * d, j, xyzw, row_v[d][window(1, d, j)], ratio, jumps[d])
-        for c in range(COLS):
+    for d in (0, 1):
+        ghost_second(d, slice(1, 3), (0, COLS + 1))
+        for c in outer:
             reduce(d, 2 * d, c)
-
-    near_row(ghost_reduce)
-    last_row(ghost_reduce)
 
     for r in range(ROWS):
         def row_of(k):

time: 31.5 us -> 31.6 us (level)
  no operation moved by 1% of the time
where the time goes in v7:
time: 31.6 us; the launch traced here: 31.4 us
  Pallas kernels  30.1 us (95%)
  between operations  1.29 us (4%)
    pallas_call x1, Pallas kernels, local(): pl.pallas_call(functools.partial(kernel, ny, nx), out_shape=(jax.ShapeDty...  29.5 us

profile of v7, /device:TPU:7, one launch (start us, length us, event | category | flops | bytes accessed | tf_op | source)
XLA Modules:
  0.0 31.4 jit_solution(6037974640206607607)
XLA Ops:
  1.3 29.5 %sph_step.1 = (f32[2,8,128]{2,1,0:T(8,128)S(1)}, f32[2,3,8,128]{3,2,1,0:T(8,128)S(1)}) custom-call(s32[2,8]{1,0:T(2,128)} %counts_in.1, s32[1]{0:T(128)S(6)} %copy.7.shift, f32[2,3,8,128]{3,2,1,0:T(8,128)} %bitcast.3, f32[2,3,8,128]{3,2,1,0:T(8,128)} %bitcast.4, f32[2,8,128]{2,1,0:T(8,128)} %mass_in.1), custom_call_target="tpu_custom_call" | custom-call | tf_op jit(solution)/shard_map/sph_step/pallas_call | solution.py:459
  30.8 0.6 %put_out.1 = (f32[2,8,128]{2,1,0:T(8,128)}, f32[2,3,8,128]{3,2,1,0:T(8,128)}) custom-call(f32[2,8,128]{2,1,0:T(8,128)S(1)} %get-tuple-element.6.density, f32[2,3,8,128]{3,2,1,0:T(8,128)S(1)} %get-tuple-element.7.accel), custom_call_target="tpu_custom_call" | custom-call | tf_op jit(solution)/shard_map/put_out/pallas_call | solution.py:498

commit v8 on v7

--- a/solution.py
+++ b/solution.py
@@ -150,18 +150,13 @@
         bound = jnp.concatenate([jnp.full((1, SLOTS), counts[r, c], jnp.int32) for c in range(COLS)], axis=0)
         return lane < bound
 
-    for load in loads:
+    for load in loads[:3]:
         load.wait()
     for r in range(ROWS):
         fields = [pos[r, 0], pos[r, 1], pos[r, 2], jnp.where(valid_of(r), mass[r], 0.0)]
         for f in range(4):
             for c in range(COLS):
                 own_a[r, c, f : f + 1, :] = fields[f][c : c + 1, :]
-        for f in range(3):
-            for c in range(COLS):
-                own_v[r, c, f : f + 1, :] = vel[r, f][c : c + 1, :]
-        for c in range(COLS):
-            own_v[r, c, 3:4, :] = zeros(1)
 
     def scaled(xyzw, j, row):
         row = row.astype(F32) if hasattr(row, "astype") else float(row)
@@ -205,6 +200,13 @@
         start(sent_a)
         pl.when(top == 1)(lambda: start(sent_up))
         pl.when(bottom == 1)(lambda: start(sent_down))
+        loads[3].wait()
+        for r in range(ROWS):
+            for f in range(3):
+                for c in range(COLS):
+                    own_v[r, c, f : f + 1, :] = vel[r, f][c : c + 1, :]
+            for c in range(COLS):
+                own_v[r, c, 3:4, :] = zeros(1)
         start(sent_v)
 
     first = (nx - gx) // nx

time: 31.6 us -> 31.6 us (level)
  no operation moved by 1% of the time
where the time goes in v8:
time: 31.6 us; the launch traced here: 31.4 us
  Pallas kernels  30.1 us (95%)
  between operations  1.29 us (4%)
    pallas_call x1, Pallas kernels, local(): pl.pallas_call(functools.partial(kernel, ny, nx), out_shape=(jax.ShapeDty...  29.5 us

profile of v8, /device:TPU:7, one launch (start us, length us, event | category | flops | bytes accessed | tf_op | source)
XLA Modules:
  0.0 31.4 jit_solution(11886536946514809809)
XLA Ops:
  1.3 29.5 %sph_step.1 = (f32[2,8,128]{2,1,0:T(8,128)S(1)}, f32[2,3,8,128]{3,2,1,0:T(8,128)S(1)}) custom-call(s32[2,8]{1,0:T(2,128)} %counts_in.1, s32[1]{0:T(128)S(6)} %copy.7.shift, f32[2,3,8,128]{3,2,1,0:T(8,128)} %bitcast.3, f32[2,3,8,128]{3,2,1,0:T(8,128)} %bitcast.4, f32[2,8,128]{2,1,0:T(8,128)} %mass_in.1), custom_call_target="tpu_custom_call" | custom-call | tf_op jit(solution)/shard_map/sph_step/pallas_call | solution.py:461
  30.8 0.6 %put_out.1 = (f32[2,8,128]{2,1,0:T(8,128)}, f32[2,3,8,128]{3,2,1,0:T(8,128)}) custom-call(f32[2,8,128]{2,1,0:T(8,128)S(1)} %get-tuple-element.6.density, f32[2,3,8,128]{3,2,1,0:T(8,128)S(1)} %get-tuple-element.7.accel), custom_call_target="tpu_custom_call" | custom-call | tf_op jit(solution)/shard_map/put_out/pallas_call | solution.py:500
